TPU v7x, 32 devices: a whole 2x2x4 slice. The times are simulated.
32 devices in a mesh: gx: 16 (over z, y, core), gy: 2 (over x).
Axes of the slice: x: 2, y: 2, z: 4, core: 2. Of those that a mesh axis runs over, the one named last changes fastest.
Arguments:
- right_side: float32 [16, 2, 512, 256], P('gx', 'gy'), may hold values from -8 to 8, as said below
- coords: float32 [16, 2, 2, 512], P('gx', 'gy'), may hold values from 0 to 1
- noise: float32 [16, 2, 512], P('gx', 'gy'), may hold values from 0.25 to 1
- intersect: int32 [16, 2, 128], P('gx', 'gy'), may hold values from 0 to 4607, as said below
Outputs:
- solution: float32 [16, 2, 512, 256], P('gx', 'gy')
- residual: float32 [16, 2, 512, 256], P('gx', 'gy')
Inputs may be any that keep to these rules, and one draw needn't show every extreme that they name: `right_side`: right-hand sides of order one. `intersect`: each subdomain's list holds 128 distinct indices in increasing order; none names the subdomain itself (block number 4) or a subdomain beyond the first or last one along the second dimension.
All inputs are finite; a program needn't handle non-finite values.
Results may differ from a plain program's by a relative error of at most 0.0003.
Values sent between devices are 32-bit elements; how exact they have to be, the bound alone decides.
No kernel may reach another device: no remote copies, remote signals or barrier semaphores. Data moves between devices by JAX's collectives and lax.ppermute only.
A program may use at most 128 MiB of HBM per device.

v0:
```python
import math

import jax
import jax.numpy as jnp
from jax import lax
from jax.sharding import PartitionSpec as P

ITERS = 3


RANGE_LEN = 0.25
ROOT_THREE = math.sqrt(3.0)
HIGH = lax.Precision.HIGHEST


def shifted(value, axis, by):
    count = lax.axis_size(axis)
    return lax.ppermute(value, axis, [(i, (i + by) % count) for i in range(count)])


def passed_along(block, axis, distance):
    devices = range(lax.axis_size(axis))
    route = [(i - distance, i) for i in devices if i - distance in devices]
    return lax.ppermute(block, axis, route)


def kernel_block(rows_pos, cols_pos):
    delta_x = rows_pos[0][:, None] - cols_pos[0][None, :]
    delta_y = rows_pos[1][:, None] - cols_pos[1][None, :]
    distance = jnp.sqrt(delta_x * delta_x + delta_y * delta_y)
    scaled = ROOT_THREE / RANGE_LEN * distance
    clipped = jnp.minimum(distance, 1.0)
    taper_val = jnp.square(jnp.square(1.0 - clipped)) * (4.0 * clipped + 1.0)
    return (1.0 + scaled) * jnp.exp(-scaled) * taper_val


def window_values(values):
    beside = {}
    for step_by in (1, -1):
        beside[step_by] = shifted(values, "gx", step_by)
    column = jnp.stack([beside[1], values, beside[-1]])
    across = {}
    for step_by in (1, -1):
        across[step_by] = passed_along(column, "gy", step_by)
    return [across[1], column, across[-1]]


def window_index(values):
    beside = {}
    for step_by in (1, -1):
        beside[step_by] = shifted(values, "gx", step_by)
    column = jnp.stack([beside[1], values, beside[-1]])
    across = {}
    for step_by in (1, -1):
        across[step_by] = passed_along(column, "gy", step_by)
    return [across[1], column, across[-1]]


def column_sum(first, second):
    return jnp.sum(first * second, axis=0)


def residual_dot(residue, precond):
    return lax.psum(column_sum(residue, precond), ("gx", "gy"))


def shards(right_side, coords, noise, intersect):
    points = right_side.shape[2]
    rhs_count = right_side.shape[3]
    intersect_len = intersect.shape[2]
    ext_len = points + intersect_len
    own_pos = coords.reshape(2, points)
    own_noise = noise.reshape(points)
    point_info = jnp.concatenate([own_pos, own_noise[None, :]], axis=0)
    info_cols = window_values(point_info)
    positions = [
        [
            jnp.stack(
                [
                    info_cols[col_off][row_off, 0] + float(row_off - 1),
                    info_cols[col_off][row_off, 1] + float(col_off - 1),
                ]
            )
            for col_off in range(3)
        ]
        for row_off in range(3)
    ]
    intersect_ids = intersect.reshape(intersect_len)
    block_id = intersect_ids // points
    row_in = intersect_ids % points
    row_of = block_id // 3
    col_of = block_id % 3
    local_id = row_of * points + row_in
    picked_info = [
        jnp.take(
            jnp.transpose(info_cols[col_off], (1, 0, 2)).reshape(3, 3 * points), local_id, axis=1
        )
        for col_off in range(3)
    ]
    chosen = jnp.where(
        col_of[None, :] == 0,
        picked_info[0],
        jnp.where(col_of[None, :] == 1, picked_info[1], picked_info[2]),
    )
    ov_pos = jnp.stack(
        [chosen[0] + (row_of - 1).astype(jnp.float32), chosen[1] + (col_of - 1).astype(jnp.float32)]
    )
    ext_pos = jnp.concatenate([own_pos, ov_pos], axis=1)
    ext_noise = jnp.concatenate([own_noise, chosen[2]])
    local_matrix = kernel_block(ext_pos, ext_pos) + jnp.diag(ext_noise)
    factor = jnp.linalg.cholesky(local_matrix)
    inv_factor = lax.linalg.triangular_solve(
        factor, jnp.eye(ext_len, dtype=jnp.float32), left_side=True, lower=True
    )
    inverse = jnp.dot(inv_factor.T, inv_factor, precision=HIGH, preferred_element_type=jnp.float32)
    near_ids = window_index(intersect_ids)
    point_iota = jnp.arange(points, dtype=jnp.int32)[:, None]
    row_base = (2 - jnp.arange(3, dtype=jnp.int32))[:, None] * 3
    selectors = []
    for col_off in range(3):
        own_rows = near_ids[col_off] - (row_base + (2 - col_off)) * points
        selectors.append((point_iota == own_rows.reshape(1, 3 * intersect_len)).astype(jnp.float32))

    def borrowed_rows(residue):
        requested = [
            lax.dot_general(
                selectors[col_off],
                residue,
                (((0,), (0,)), ((), ())),
                precision=HIGH,
                preferred_element_type=jnp.float32,
            ).reshape(3, intersect_len, rhs_count)
            for col_off in range(3)
        ]
        combined = jnp.stack([requested[col_off][1] for col_off in range(3)])
        for step_by, row_off in ((-1, 0), (1, 2)):
            outgoing = jnp.stack([requested[col_off][row_off] for col_off in range(3)])
            combined = combined + shifted(outgoing, "gx", step_by)
        gathered = combined[1]
        for step_by, col_off in ((-1, 0), (1, 2)):
            gathered = gathered + passed_along(combined[col_off], "gy", step_by)
        return gathered

    def precondition(residue):
        gathered = borrowed_rows(residue)
        extended = jnp.concatenate([residue, gathered], axis=0)
        solved = jnp.dot(inverse, extended, precision=HIGH, preferred_element_type=jnp.float32)
        returned = window_values(solved[points:])
        result = solved[:points]
        for col_off in range(3):
            result = result + jnp.dot(
                selectors[col_off],
                returned[col_off].reshape(3 * intersect_len, rhs_count),
                precision=HIGH,
                preferred_element_type=jnp.float32,
            )
        return result

    noise_col = own_noise[:, None]
    residual = right_side.reshape(points, rhs_count)
    solution = jnp.zeros_like(residual)
    precond = precondition(residual)
    direction = precond
    inner_now = residual_dot(residual, precond)
    for iteration in range(ITERS):
        columns = window_values(direction)
        accumulated = noise_col * direction
        for operate_row_off in range(3):
            for operate_col_off in range(3):
                accumulated = accumulated + jnp.dot(
                    kernel_block(own_pos, positions[operate_row_off][operate_col_off]),
                    columns[operate_col_off][operate_row_off],
                    precision=HIGH,
                    preferred_element_type=jnp.float32,
                )
        step_size = inner_now / lax.psum(column_sum(direction, accumulated), ("gx", "gy"))
        solution = solution + step_size * direction
        residual = residual - step_size * accumulated
        if iteration + 1 < ITERS:
            precond = precondition(residual)
            inner_next = residual_dot(residual, precond)
            direction = precond + inner_next / inner_now * direction
            inner_now = inner_next
    return (solution.reshape(1, 1, points, rhs_count), residual.reshape(1, 1, points, rhs_count))


def solution(mesh):
    placed = (
        P("gx", "gy", None, None),
        P("gx", "gy", None, None),
        P("gx", "gy", None),
        P("gx", "gy", None),
    )
    return jax.shard_map(
        shards,
        mesh=mesh,
        in_specs=placed,
        out_specs=(P("gx", "gy", None, None), P("gx", "gy", None, None)),
        check_vma=False,
    )
```

profile of v0, /device:TPU:0, one launch (start us, length us, event | category | flops | bytes accessed | tf_op | source)
XLA Modules:
  0.0 750.6 jit_solution(9324209336027450057)
XLA Ops:
  1.2 5.0 collective-permute-start.5
  7.0 4.4 collective-permute-start.1
  15.4 4.5 collective-permute-start.6
  23.5 3.7 collective-permute-start.2
  38.7 11.7 %cholesky.132 = f32[128,128]{1,0:T(8,128)S(1)} custom-call(f32[128,128]{1,0:T(8,128)S(1)} %cholesky.337), custom_call_target="Cholesky" | custom-call | tf_op jit(solution)/shard_map/jit(cholesky)/cholesky | solution.py:111
  50.6 9.8 %custom-call.38 = f32[1,128,128]{1,2,0:T(8,128)S(1)} custom-call(f32[1,128,128]{2,1,0:T(8,128)S(1)} %get-tuple-element.83), custom_call_target="InvertDiagBlocksLowerTriangular" | custom-call | tf_op jit(solution)/shard_map/jit(cholesky)/cholesky | solution.py:111
  63.0 11.9 %cholesky.270 = f32[128,128]{1,0:T(8,128)S(1)} custom-call(f32[128,128]{1,0:T(8,128)S(1)} %cholesky.341), custom_call_target="Cholesky" | custom-call | tf_op jit(solution)/shard_map/jit(cholesky)/cholesky | solution.py:111
  76.3 9.8 %custom-call.39 = f32[1,128,128]{1,2,0:T(8,128)S(1)} custom-call(f32[1,128,128]{2,1,0:T(8,128)S(1)} %get-tuple-element.80), custom_call_target="InvertDiagBlocksLowerTriangular" | custom-call | tf_op jit(solution)/shard_map/jit(cholesky)/cholesky | solution.py:111
  87.8 11.7 %cholesky.291 = f32[128,128]{1,0:T(8,128)S(1)} custom-call(f32[128,128]{1,0:T(8,128)S(1)} %cholesky.346), custom_call_target="Cholesky" | custom-call | tf_op jit(solution)/shard_map/jit(cholesky)/cholesky | solution.py:111
  100.3 9.8 %custom-call.40 = f32[1,128,128]{1,2,0:T(8,128)S(1)} custom-call(f32[1,128,128]{2,1,0:T(8,128)S(1)} %get-tuple-element.77), custom_call_target="InvertDiagBlocksLowerTriangular" | custom-call | tf_op jit(solution)/shard_map/jit(cholesky)/cholesky | solution.py:111
  112.0 11.7 %cholesky.310 = f32[128,128]{1,0:T(8,128)S(1)} custom-call(f32[128,128]{1,0:T(8,128)S(1)} %cholesky.351), custom_call_target="Cholesky" | custom-call | tf_op jit(solution)/shard_map/jit(cholesky)/cholesky | solution.py:111
  124.4 9.8 %custom-call.41 = f32[1,128,128]{1,2,0:T(8,128)S(1)} custom-call(f32[1,128,128]{2,1,0:T(8,128)S(1)} %get-tuple-element.74), custom_call_target="InvertDiagBlocksLowerTriangular" | custom-call | tf_op jit(solution)/shard_map/jit(cholesky)/cholesky | solution.py:111
  135.7 11.7 %cholesky.327 = f32[128,128]{1,0:T(8,128)S(1)} custom-call(f32[128,128]{1,0:T(8,128)S(1)} %convolution_subtract_fusion.6), custom_call_target="Cholesky" | custom-call | tf_op jit(solution)/shard_map/jit(cholesky)/cholesky | solution.py:111
  152.5 17.8 %while.1 = (s32[]{:T(128)}, f32[640,640]{1,0:T(8,128)}, s32[5,2]{0,1:T(2,128)S(1)}, f32[5,128,128]{2,1,0:T(8,128)}, s32[]{:T(128)}) while((s32[]{:T(128)}, f32[640,640]{1,0:T(8,128)}, s32[5,2]{0,1:T(2,128)S(1)}, f32[5,128,128]{2,1,0:T(8,128)}, s32[]{:T(128)}) %tuple.96), condition=%wide.while_cond, body=%wide.while_body.sunk | while | flops 2 | bytes 132705 | solution.py:112
  170.3 50.7 %custom-call.42 = f32[5,128,128]{1,2,0:T(8,128)} custom-call(f32[5,128,128]{2,1,0:T(8,128)} %get-tuple-element.10), custom_call_target="InvertDiagBlocksLowerTriangular" | custom-call | tf_op jit(solution)/shard_map/triangular_solve | solution.py:112
  234.1 4.7 collective-permute-start.11
  238.8 5.0 fusion.240
  245.7 4.4 collective-permute-start.13
  260.4 3.8 collective-permute-done.15
  264.9 4.4 collective-permute-start.17
  269.3 7.0 collective-permute-done.16
  285.3 26.6 %collective-permute-done.18 = f32[3,512,256]{2,1,0:T(8,128)S(1)} collective-permute-done((f32[3,512,256]{2,1,0:T(8,128)S(1)}, f32[3,512,256]{2,1,0:T(8,128)S(1)}, u32[]{:S(2)}, u32[]{:S(2)}) %collective-permute-start.18) | collective-permute-done | bytes 1572896 | tf_op jit(solution)/shard_map/ppermute | solution.py:24
  324.2 41.0 %all-reduce.1 = (f32[256]{0:T(256)S(1)}, f32[256]{0:T(256)S(1)}) all-reduce(f32[256]{0:T(256)S(1)} %get-tuple-element.12, f32[256]{0:T(256)S(1)} %get-tuple-element.11), channel_id=1, replica_groups=mesh['gx'=16,'gy'=2] {'gx','gy'}, use_global_device_ids=true, to_apply=%region_11.13 | all-reduce | flops 512 | bytes 4096 | tf_op jit(solution)/shard_map/psum | solution.py:64
  369.5 5.2 collective-permute-done.20
  374.7 4.8 collective-permute-done.21
  380.9 4.6 collective-permute-start.23
  391.3 4.1 collective-permute-start.25
  398.2 4.4 collective-permute-start.26
  404.5 7.1 collective-permute-done.26
  412.3 3.5 collective-permute-done.27
  417.2 36.8 %psum.44 = f32[256]{0:T(256)S(1)} all-reduce(f32[256]{0:T(256)S(1)} %get-tuple-element.128), channel_id=1, replica_groups=mesh['gx'=16,'gy'=2] {'gx','gy'}, use_global_device_ids=true, to_apply=%region_15.17 | all-reduce | flops 256 | bytes 2048 | tf_op jit(solution)/shard_map/psum | solution.py:64
  455.2 4.4 collective-permute-start.29
  459.6 7.0 collective-permute-done.28
  466.7 4.3 collective-permute-start.30
  478.3 24.6 %collective-permute-done.30 = f32[3,512,256]{2,1,0:T(8,128)S(1)} collective-permute-done((f32[3,512,256]{2,1,0:T(8,128)S(1)}, f32[3,512,256]{2,1,0:T(8,128)S(1)}, u32[]{:S(2)}, u32[]{:S(2)}) %collective-permute-start.30) | collective-permute-done | bytes 1572896 | tf_op jit(solution)/shard_map/ppermute | solution.py:24
  515.2 43.2 %psum.45 = f32[256]{0:T(256)S(1)} all-reduce(f32[256]{0:T(256)S(1)} %get-tuple-element.130), channel_id=1, replica_groups=mesh['gx'=16,'gy'=2] {'gx','gy'}, use_global_device_ids=true, to_apply=%region_17.19 | all-reduce | flops 256 | bytes 2048 | tf_op jit(solution)/shard_map/psum | solution.py:176
  562.8 5.2 collective-permute-done.32
  568.0 4.8 collective-permute-done.33
  574.2 4.6 collective-permute-start.35
  584.5 4.1 collective-permute-start.37
  591.4 4.4 collective-permute-start.38
  597.8 6.8 collective-permute-done.38
  609.4 36.9 %psum.46 = f32[256]{0:T(256)S(1)} all-reduce(f32[256]{0:T(256)S(1)} %get-tuple-element.132), channel_id=1, replica_groups=mesh['gx'=16,'gy'=2] {'gx','gy'}, use_global_device_ids=true, to_apply=%region_19.21 | all-reduce | flops 256 | bytes 2048 | tf_op jit(solution)/shard_map/psum | solution.py:64
  646.4 4.4 collective-permute-start.41
  650.8 7.0 collective-permute-done.40
  657.9 4.3 collective-permute-start.42
  669.3 25.0 %collective-permute-done.42 = f32[3,512,256]{2,1,0:T(8,128)S(1)} collective-permute-done((f32[3,512,256]{2,1,0:T(8,128)S(1)}, f32[3,512,256]{2,1,0:T(8,128)S(1)}, u32[]{:S(2)}, u32[]{:S(2)}) %collective-permute-start.42) | collective-permute-done | bytes 1572896 | tf_op jit(solution)/shard_map/ppermute | solution.py:24
  705.9 43.1 %psum.47 = f32[256]{0:T(256)S(1)} all-reduce(f32[256]{0:T(256)S(1)} %get-tuple-element.134), channel_id=1, replica_groups=mesh['gx'=16,'gy'=2] {'gx','gy'}, use_global_device_ids=true, to_apply=%region_21.23 | all-reduce | flops 256 | bytes 2048 | tf_op jit(solution)/shard_map/psum | solution.py:176
  (255 shorter events, 177.0 us)
Async XLA Ops:
  0.6 19.3 %copy-start = (f32[1,1,512,256]{3,2,1,0:T(8,128)S(1)}, f32[1,1,512,256]{3,2,1,0:T(8,128)}, u32[]{:S(2)}) copy-start(f32[1,1,512,256]{3,2,1,0:T(8,128)} %param.6) | copy-start | bytes 1572868
  0.7 13.4 %collective-permute-start.4 = (s32[128]{0:T(128)}, s32[128]{0:T(128)S(1)}, u32[]{:S(2)}, u32[]{:S(2)}) collective-permute-start(s32[128]{0:T(128)} %bitcast.373), channel_id=1, source_target_pairs={{0,2},{2,4},{4,6},{6,8},{8,10},{10,12},{12,14},{14,16},{16,18},{18... | collective-permute-start | bytes 1544 | tf_op jit(solution)/shard_map/ppermute | solution.py:18
  1.2 12.8 %collective-permute-start.5 = (s32[128]{0:T(128)}, s32[128]{0:T(128)S(1)}, u32[]{:S(2)}, u32[]{:S(2)}) collective-permute-start(s32[128]{0:T(128)} %bitcast.374), channel_id=1, source_target_pairs={{0,30},{2,0},{4,2},{6,4},{8,6},{10,8},{12,10},{14,12},{16,14},{18,... | collective-permute-start | bytes 1544 | tf_op jit(solution)/shard_map/ppermute | solution.py:18
  7.0 16.5 %collective-permute-start = (f32[3,512]{1,0:T(4,128)S(1)}, f32[3,512]{1,0:T(4,128)S(1)}, u32[]{:S(2)}, u32[]{:S(2)}) collective-permute-start(f32[3,512]{1,0:T(4,128)S(1)} %get-tuple-element.110), channel_id=1, source_target_pairs={{0,2},{2,4},{4,6},{6,8},{8,10},{10,12},{12,14},{14,16},{16,18},{18... | collective-permute-start | bytes 18440 | tf_op jit(solution)/shard_map/ppermute | solution.py:18
  7.0 16.4 %collective-permute-start.1 = (f32[3,512]{1,0:T(4,128)S(1)}, f32[3,512]{1,0:T(4,128)S(1)}, u32[]{:S(2)}, u32[]{:S(2)}) collective-permute-start(f32[3,512]{1,0:T(4,128)S(1)} %get-tuple-element.110), channel_id=1, source_target_pairs={{0,30},{2,0},{4,2},{6,4},{8,6},{10,8},{12,10},{14,12},{16,14},{18,... | collective-permute-start | bytes 18440 | tf_op jit(solution)/shard_map/ppermute | solution.py:18
  14.1 6.7 collective-permute-start.7
  15.4 6.3 collective-permute-start.6
  23.5 208.1 %collective-permute-start.8 = (f32[3,128,256]{2,1,0:T(8,128)}, f32[3,128,256]{2,1,0:T(8,128)}, u32[]{:S(2)}, u32[]{:S(2)}) collective-permute-start(f32[3,128,256]{2,1,0:T(8,128)} %pad_maximum_fusion.3), channel_id=1, source_target_pairs={{0,30},{2,0},{4,2},{6,4},{8,6},{10,8},{12,10},{14,12},{16,14},{18,... | collective-permute-start | bytes 1179656 | tf_op jit(solution)/shard_map/ppermute | solution.py:18
  23.5 7.5 collective-permute-start.2
  27.2 5.7 collective-permute-start.3
  29.3 202.3 %collective-permute-start.9 = (f32[3,128,256]{2,1,0:T(8,128)}, f32[3,128,256]{2,1,0:T(8,128)}, u32[]{:S(2)}, u32[]{:S(2)}) collective-permute-start(f32[3,128,256]{2,1,0:T(8,128)} %pad_maximum_fusion.4), channel_id=1, source_target_pairs={{0,2},{2,4},{4,6},{6,8},{8,10},{10,12},{12,14},{14,16},{16,18},{18... | collective-permute-start | bytes 1179656 | tf_op jit(solution)/shard_map/ppermute | solution.py:18
  170.3 54.7 %copy-start.3 = (f32[640,640]{1,0:T(8,128)S(1)}, f32[640,640]{1,0:T(8,128)}, u32[]{:S(2)}) copy-start(f32[640,640]{1,0:T(8,128)} %fusion.25) | copy-start | bytes 4915204
  232.8 11.1 %collective-permute-start.10 = (f32[128,256]{1,0:T(8,128)S(1)}, f32[128,256]{1,0:T(8,128)S(1)}, u32[]{:S(2)}, u32[]{:S(2)}) collective-permute-start(f32[128,256]{1,0:T(8,128)S(1)} %get-tuple-element.60), channel_id=1, source_target_pairs={{1,0},{3,2},{5,4},{7,6},{9,8},{11,10},{13,12},{15,14},{17,16},{19,... | collective-permute-start | bytes 393224 | tf_op jit(solution)/shard_map/ppermute | solution.py:24
  234.1 9.8 %collective-permute-start.11 = (f32[128,256]{1,0:T(8,128)S(1)}, f32[128,256]{1,0:T(8,128)S(1)}, u32[]{:S(2)}, u32[]{:S(2)}) collective-permute-start(f32[128,256]{1,0:T(8,128)S(1)} %get-tuple-element.61), channel_id=1, source_target_pairs={{0,1},{2,3},{4,5},{6,7},{8,9},{10,11},{12,13},{14,15},{16,17},{18,... | collective-permute-start | bytes 393224 | tf_op jit(solution)/shard_map/ppermute | solution.py:24
  245.7 7.1 collective-permute-start.12
  245.7 7.1 collective-permute-start.13
  252.9 6.9 collective-permute-start.14
  254.5 9.7 %collective-permute-start.15 = (f32[3,128,256]{2,1,0:T(8,128)S(1)}, f32[3,128,256]{2,1,0:T(8,128)S(1)}, u32[]{:S(2)}, u32[]{:S(2)}) collective-permute-start(f32[3,128,256]{2,1,0:T(8,128)S(1)} %pad_maximum_fusion.5), channel_id=1, source_target_pairs={{1,0},{3,2},{5,4},{7,6},{9,8},{11,10},{13,12},{15,14},{17,16},{19,... | collective-permute-start | bytes 1179656 | tf_op jit(solution)/shard_map/ppermute | solution.py:24
  264.8 11.5 %collective-permute-start.16 = (f32[512,256]{1,0:T(8,128)S(1)}, f32[512,256]{1,0:T(8,128)S(1)}, u32[]{:S(2)}, u32[]{:S(2)}) collective-permute-start(f32[512,256]{1,0:T(8,128)S(1)} %convolution_add_fusion.5), channel_id=1, source_target_pairs={{0,2},{2,4},{4,6},{6,8},{8,10},{10,12},{12,14},{14,16},{16,18},{18... | collective-permute-start | bytes 1572872 | tf_op jit(solution)/shard_map/ppermute | solution.py:18
  264.9 11.4 %collective-permute-start.17 = (f32[512,256]{1,0:T(8,128)S(1)}, f32[512,256]{1,0:T(8,128)S(1)}, u32[]{:S(2)}, u32[]{:S(2)}) collective-permute-start(f32[512,256]{1,0:T(8,128)S(1)} %convolution_add_fusion.5), channel_id=1, source_target_pairs={{0,30},{2,0},{4,2},{6,4},{8,6},{10,8},{12,10},{14,12},{16,14},{18,... | collective-permute-start | bytes 1572872 | tf_op jit(solution)/shard_map/ppermute | solution.py:18
  276.4 35.5 %collective-permute-start.18 = (f32[3,512,256]{2,1,0:T(8,128)S(1)}, f32[3,512,256]{2,1,0:T(8,128)S(1)}, u32[]{:S(2)}, u32[]{:S(2)}) collective-permute-start(f32[3,512,256]{2,1,0:T(8,128)S(1)} %pad_maximum_fusion), channel_id=1, source_target_pairs={{0,1},{2,3},{4,5},{6,7},{8,9},{10,11},{12,13},{14,15},{16,17},{18,... | collective-permute-start | bytes 4718600 | tf_op jit(solution)/shard_map/ppermute | solution.py:24
  278.0 39.4 %collective-permute-start.19 = (f32[3,512,256]{2,1,0:T(8,128)S(1)}, f32[3,512,256]{2,1,0:T(8,128)S(1)}, u32[]{:S(2)}, u32[]{:S(2)}) collective-permute-start(f32[3,512,256]{2,1,0:T(8,128)S(1)} %pad_maximum_fusion), channel_id=1, source_target_pairs={{1,0},{3,2},{5,4},{7,6},{9,8},{11,10},{13,12},{15,14},{17,16},{19,... | collective-permute-start | bytes 4718600 | tf_op jit(solution)/shard_map/ppermute | solution.py:24
  368.9 5.8 collective-permute-start.20
  369.5 10.1 %collective-permute-start.21 = (f32[3,128,256]{2,1,0:T(8,128)S(1)}, f32[3,128,256]{2,1,0:T(8,128)S(1)}, u32[]{:S(2)}, u32[]{:S(2)}) collective-permute-start(f32[3,128,256]{2,1,0:T(8,128)S(1)} %pad_maximum_fusion.7), channel_id=1, source_target_pairs={{0,2},{2,4},{4,6},{6,8},{8,10},{10,12},{12,14},{14,16},{16,18},{18... | collective-permute-start | bytes 1179656 | tf_op jit(solution)/shard_map/ppermute | solution.py:18
  379.6 7.7 %collective-permute-start.22 = (f32[128,256]{1,0:T(8,128)S(1)}, f32[128,256]{1,0:T(8,128)S(1)}, u32[]{:S(2)}, u32[]{:S(2)}) collective-permute-start(f32[128,256]{1,0:T(8,128)S(1)} %get-tuple-element.49), channel_id=1, source_target_pairs={{1,0},{3,2},{5,4},{7,6},{9,8},{11,10},{13,12},{15,14},{17,16},{19,... | collective-permute-start | bytes 393224 | tf_op jit(solution)/shard_map/ppermute | solution.py:24
  380.9 8.2 %collective-permute-start.23 = (f32[128,256]{1,0:T(8,128)S(1)}, f32[128,256]{1,0:T(8,128)S(1)}, u32[]{:S(2)}, u32[]{:S(2)}) collective-permute-start(f32[128,256]{1,0:T(8,128)S(1)} %get-tuple-element.50), channel_id=1, source_target_pairs={{0,1},{2,3},{4,5},{6,7},{8,9},{10,11},{12,13},{14,15},{16,17},{18,... | collective-permute-start | bytes 393224 | tf_op jit(solution)/shard_map/ppermute | solution.py:24
  390.9 7.2 collective-permute-start.24
  391.3 6.8 collective-permute-start.25
  398.2 13.5 %collective-permute-start.26 = (f32[3,128,256]{2,1,0:T(8,128)S(1)}, f32[3,128,256]{2,1,0:T(8,128)S(1)}, u32[]{:S(2)}, u32[]{:S(2)}) collective-permute-start(f32[3,128,256]{2,1,0:T(8,128)S(1)} %pad_maximum_fusion.8), channel_id=1, source_target_pairs={{0,1},{2,3},{4,5},{6,7},{8,9},{10,11},{12,13},{14,15},{16,17},{18,... | collective-permute-start | bytes 1179656 | tf_op jit(solution)/shard_map/ppermute | solution.py:24
  402.6 13.2 %collective-permute-start.27 = (f32[3,128,256]{2,1,0:T(8,128)S(1)}, f32[3,128,256]{2,1,0:T(8,128)S(1)}, u32[]{:S(2)}, u32[]{:S(2)}) collective-permute-start(f32[3,128,256]{2,1,0:T(8,128)S(1)} %pad_maximum_fusion.8), channel_id=1, source_target_pairs={{1,0},{3,2},{5,4},{7,6},{9,8},{11,10},{13,12},{15,14},{17,16},{19,... | collective-permute-start | bytes 1179656 | tf_op jit(solution)/shard_map/ppermute | solution.py:24
  455.1 57.2 %copy-start.1 = (f32[512,256]{1,0:T(8,128)}, f32[512,256]{1,0:T(8,128)S(1)}, u32[]{:S(2)}) copy-start(f32[512,256]{1,0:T(8,128)S(1)} %multiply_add_fusion.1) | copy-start | bytes 1572868
  455.1 11.5 %collective-permute-start.28 = (f32[512,256]{1,0:T(8,128)S(1)}, f32[512,256]{1,0:T(8,128)S(1)}, u32[]{:S(2)}, u32[]{:S(2)}) collective-permute-start(f32[512,256]{1,0:T(8,128)S(1)} %multiply_add_fusion.1), channel_id=1, source_target_pairs={{0,2},{2,4},{4,6},{6,8},{8,10},{10,12},{12,14},{14,16},{16,18},{18... | collective-permute-start | bytes 1572872 | tf_op jit(solution)/shard_map/ppermute | solution.py:18
  455.2 11.4 %collective-permute-start.29 = (f32[512,256]{1,0:T(8,128)S(1)}, f32[512,256]{1,0:T(8,128)S(1)}, u32[]{:S(2)}, u32[]{:S(2)}) collective-permute-start(f32[512,256]{1,0:T(8,128)S(1)} %multiply_add_fusion.1), channel_id=1, source_target_pairs={{0,30},{2,0},{4,2},{6,4},{8,6},{10,8},{12,10},{14,12},{16,14},{18,... | collective-permute-start | bytes 1572872 | tf_op jit(solution)/shard_map/ppermute | solution.py:18
  466.7 36.1 %collective-permute-start.30 = (f32[3,512,256]{2,1,0:T(8,128)S(1)}, f32[3,512,256]{2,1,0:T(8,128)S(1)}, u32[]{:S(2)}, u32[]{:S(2)}) collective-permute-start(f32[3,512,256]{2,1,0:T(8,128)S(1)} %pad_maximum_fusion.1), channel_id=1, source_target_pairs={{0,1},{2,3},{4,5},{6,7},{8,9},{10,11},{12,13},{14,15},{16,17},{18,... | collective-permute-start | bytes 4718600 | tf_op jit(solution)/shard_map/ppermute | solution.py:24
  471.0 37.4 %collective-permute-start.31 = (f32[3,512,256]{2,1,0:T(8,128)S(1)}, f32[3,512,256]{2,1,0:T(8,128)S(1)}, u32[]{:S(2)}, u32[]{:S(2)}) collective-permute-start(f32[3,512,256]{2,1,0:T(8,128)S(1)} %pad_maximum_fusion.1), channel_id=1, source_target_pairs={{1,0},{3,2},{5,4},{7,6},{9,8},{11,10},{13,12},{15,14},{17,16},{19,... | collective-permute-start | bytes 4718600 | tf_op jit(solution)/shard_map/ppermute | solution.py:24
  562.1 5.9 collective-permute-start.32
  562.7 10.1 %collective-permute-start.33 = (f32[3,128,256]{2,1,0:T(8,128)S(1)}, f32[3,128,256]{2,1,0:T(8,128)S(1)}, u32[]{:S(2)}, u32[]{:S(2)}) collective-permute-start(f32[3,128,256]{2,1,0:T(8,128)S(1)} %pad_maximum_fusion.10), channel_id=1, source_target_pairs={{0,2},{2,4},{4,6},{6,8},{8,10},{10,12},{12,14},{14,16},{16,18},{18... | collective-permute-start | bytes 1179656 | tf_op jit(solution)/shard_map/ppermute | solution.py:18
  572.9 7.8 %collective-permute-start.34 = (f32[128,256]{1,0:T(8,128)S(1)}, f32[128,256]{1,0:T(8,128)S(1)}, u32[]{:S(2)}, u32[]{:S(2)}) collective-permute-start(f32[128,256]{1,0:T(8,128)S(1)} %get-tuple-element.38), channel_id=1, source_target_pairs={{1,0},{3,2},{5,4},{7,6},{9,8},{11,10},{13,12},{15,14},{17,16},{19,... | collective-permute-start | bytes 393224 | tf_op jit(solution)/shard_map/ppermute | solution.py:24
  574.2 8.2 %collective-permute-start.35 = (f32[128,256]{1,0:T(8,128)S(1)}, f32[128,256]{1,0:T(8,128)S(1)}, u32[]{:S(2)}, u32[]{:S(2)}) collective-permute-start(f32[128,256]{1,0:T(8,128)S(1)} %get-tuple-element.39), channel_id=1, source_target_pairs={{0,1},{2,3},{4,5},{6,7},{8,9},{10,11},{12,13},{14,15},{16,17},{18,... | collective-permute-start | bytes 393224 | tf_op jit(solution)/shard_map/ppermute | solution.py:24
  584.1 7.2 collective-permute-start.36
  584.5 6.9 collective-permute-start.37
  591.4 13.1 %collective-permute-start.38 = (f32[3,128,256]{2,1,0:T(8,128)S(1)}, f32[3,128,256]{2,1,0:T(8,128)S(1)}, u32[]{:S(2)}, u32[]{:S(2)}) collective-permute-start(f32[3,128,256]{2,1,0:T(8,128)S(1)} %pad_maximum_fusion.11), channel_id=1, source_target_pairs={{0,1},{2,3},{4,5},{6,7},{8,9},{10,11},{12,13},{14,15},{16,17},{18,... | collective-permute-start | bytes 1179656 | tf_op jit(solution)/shard_map/ppermute | solution.py:24
  595.8 12.8 %collective-permute-start.39 = (f32[3,128,256]{2,1,0:T(8,128)S(1)}, f32[3,128,256]{2,1,0:T(8,128)S(1)}, u32[]{:S(2)}, u32[]{:S(2)}) collective-permute-start(f32[3,128,256]{2,1,0:T(8,128)S(1)} %pad_maximum_fusion.11), channel_id=1, source_target_pairs={{1,0},{3,2},{5,4},{7,6},{9,8},{11,10},{13,12},{15,14},{17,16},{19,... | collective-permute-start | bytes 1179656 | tf_op jit(solution)/shard_map/ppermute | solution.py:24
  605.2 41.1 %copy-start.2 = (f32[512,256]{1,0:T(8,128)S(1)}, f32[512,256]{1,0:T(8,128)}, u32[]{:S(2)}) copy-start(f32[512,256]{1,0:T(8,128)} %copy-done.1) | copy-start | bytes 1572868
  646.3 11.5 %collective-permute-start.40 = (f32[512,256]{1,0:T(8,128)S(1)}, f32[512,256]{1,0:T(8,128)S(1)}, u32[]{:S(2)}, u32[]{:S(2)}) collective-permute-start(f32[512,256]{1,0:T(8,128)S(1)} %multiply_add_fusion), channel_id=1, source_target_pairs={{0,2},{2,4},{4,6},{6,8},{8,10},{10,12},{12,14},{14,16},{16,18},{18... | collective-permute-start | bytes 1572872 | tf_op jit(solution)/shard_map/ppermute | solution.py:18
  646.4 11.4 %collective-permute-start.41 = (f32[512,256]{1,0:T(8,128)S(1)}, f32[512,256]{1,0:T(8,128)S(1)}, u32[]{:S(2)}, u32[]{:S(2)}) collective-permute-start(f32[512,256]{1,0:T(8,128)S(1)} %multiply_add_fusion), channel_id=1, source_target_pairs={{0,30},{2,0},{4,2},{6,4},{8,6},{10,8},{12,10},{14,12},{16,14},{18,... | collective-permute-start | bytes 1572872 | tf_op jit(solution)/shard_map/ppermute | solution.py:18
  657.9 36.3 %collective-permute-start.42 = (f32[3,512,256]{2,1,0:T(8,128)S(1)}, f32[3,512,256]{2,1,0:T(8,128)S(1)}, u32[]{:S(2)}, u32[]{:S(2)}) collective-permute-start(f32[3,512,256]{2,1,0:T(8,128)S(1)} %pad_maximum_fusion.2), channel_id=1, source_target_pairs={{0,1},{2,3},{4,5},{6,7},{8,9},{10,11},{12,13},{14,15},{16,17},{18,... | collective-permute-start | bytes 4718600 | tf_op jit(solution)/shard_map/ppermute | solution.py:24
  662.2 37.6 %collective-permute-start.43 = (f32[3,512,256]{2,1,0:T(8,128)S(1)}, f32[3,512,256]{2,1,0:T(8,128)S(1)}, u32[]{:S(2)}, u32[]{:S(2)}) collective-permute-start(f32[3,512,256]{2,1,0:T(8,128)S(1)} %pad_maximum_fusion.2), channel_id=1, source_target_pairs={{1,0},{3,2},{5,4},{7,6},{9,8},{11,10},{13,12},{15,14},{17,16},{19,... | collective-permute-start | bytes 4718600 | tf_op jit(solution)/shard_map/ppermute | solution.py:24
  (5 other events, 28.6 us)
where the time goes:
time: 756 us; the launch traced here: 751 us
  blocking collectives  201 us (27%)
  other arithmetic  168 us (22%)
  waiting for transfers between devices  161 us (21%)
  starting transfers between devices  96.9 us (13%)
  matrix products  94.8 us (13%)
  local copies, waits for them, and re-layouts  22.5 us (3%)
    psum x3, blocking collectives, residual_dot(): return lax.psum(column_sum(residue, precond), ('gx', 'gy'))  115 us
    ppermute x22, waiting for transfers between devices, passed_along(): return lax.ppermute(block, axis, route)  112 us
    another operation x19, other arithmetic, shards(): factor = jnp.linalg.cholesky(local_matrix)  101 us
    psum x2, blocking collectives, shards(): lax.psum(column_sum(direction, accumulated), ('gx', 'gy'))  86.3 us
    ppermute x22, starting transfers between devices, passed_along(): return lax.ppermute(block, axis, route)  57.9 us
    dot_general x27, matrix products, shards(): jnp.dot(kernel_block(own_pos, positions[operate_row_off][operate_col_off]...  52.9 us
    another operation x3, other arithmetic, shards(): lax.linalg.triangular_solve(factor, jnp.eye(ext_len, dtype=jnp.float32),...  52 us
    ppermute x22, waiting for transfers between devices, shifted(): lax.ppermute(value, axis, [(i, (i + by) % count) for i in range(count)])  49 us
  transfers between devices with their start and end apart: 44, of which 24 were waited for; matrix products, arithmetic and copies ran while one was open for 33% of the time, Pallas kernels for 0%

commit v1 on v0

--- a/solution.py
+++ b/solution.py
@@ -3,14 +3,446 @@
 import jax
 import jax.numpy as jnp
 from jax import lax
+from jax.experimental import pallas as pl
+from jax.experimental.pallas import tpu as pltpu
 from jax.sharding import PartitionSpec as P
 
 ITERS = 3
-
-
+BASIS_SHIFT = 1.75
+NOISE_MIN = 0.25
+NOISE_MAX = 1.0
 RANGE_LEN = 0.25
 ROOT_THREE = math.sqrt(3.0)
 HIGH = lax.Precision.HIGHEST
+LANES = 128
+F32 = jnp.float32
+BF16 = jnp.bfloat16
+
+
+def params(*semantics, mib=12):
+    return pltpu.CompilerParams(
+        dimension_semantics=semantics or None, vmem_limit_bytes=mib * 2**20
+    )
+
+
+def kernel_of(delta_x, delta_y):
+    square = delta_x * delta_x + delta_y * delta_y
+    distance = square * lax.rsqrt(jnp.maximum(square, 1e-30))
+    left = jnp.maximum(1.0 - distance, 0.0)
+    quad = jnp.square(jnp.square(left))
+    rate = ROOT_THREE / RANGE_LEN
+    decay = jnp.exp2(distance * (-rate * math.log2(math.e)))
+    return ((1.0 + rate * distance) * decay) * (quad * (5.0 - 4.0 * left))
+
+
+def split(value):
+    high = value.astype(BF16)
+    return high, (value - high.astype(F32)).astype(BF16)
+
+
+def mm(first, second, **kw):
+    return jnp.dot(first, second, preferred_element_type=F32, **kw)
+
+
+def mm3(first, second):
+    first_h, first_l = split(first)
+    second_h, second_l = split(second)
+    return mm(first_h, second_h) + (mm(first_h, second_l) + mm(first_l, second_h))
+
+
+def mm4(first, second):
+    first_h, first_l = split(first)
+    second_h, second_l = split(second)
+    both = jnp.concatenate([first_h, first_l], axis=1)
+    return mm(both, jnp.concatenate([second_h, second_h], axis=0)) + mm(
+        both, jnp.concatenate([second_l, second_l], axis=0)
+    )
+
+
+def split3(value):
+    high = value.astype(BF16)
+    rest = value - high.astype(F32)
+    middle = rest.astype(BF16)
+    return high, middle, (rest - middle.astype(F32)).astype(BF16)
+
+
+def mm6(first, second):
+    fh, fm, fl = split3(first)
+    sh, sm, sl = split3(second)
+    both = jnp.concatenate([fh, fm], axis=1)
+    ends = jnp.concatenate([fh, fl], axis=1)
+    cat = lambda a, b: jnp.concatenate([a, b], axis=0)
+    return mm(both, cat(sh, sh)) + (mm(both, cat(sm, sm)) + mm(ends, cat(sl, sh)))
+
+
+def pair_of(value):
+    high, low = split(value)
+    return jnp.concatenate([high, low], axis=1)
+
+
+def folded(product):
+    half = product.shape[1] // 2
+    return product[:, :half] + product[:, half:]
+
+
+EARLY, LATE, UPDATE = mm3, mm6, mm6
+
+
+def eye_mask(size):
+    return lax.broadcasted_iota(jnp.int32, (size, size), 0) == lax.broadcasted_iota(
+        jnp.int32, (size, size), 1
+    )
+
+
+def to_col(row):
+    mask = eye_mask(LANES)
+    parts = [
+        jnp.sum(jnp.where(mask, row[:, k : k + LANES], 0.0), axis=1, keepdims=True)
+        for k in range(0, row.shape[1], LANES)
+    ]
+    return parts[0] if len(parts) == 1 else jnp.concatenate(parts, axis=0)
+
+
+def to_row(col):
+    mask = eye_mask(LANES)
+    parts = [
+        jnp.sum(jnp.where(mask, col[k : k + LANES], 0.0), axis=0, keepdims=True)
+        for k in range(0, col.shape[0], LANES)
+    ]
+    return parts[0] if len(parts) == 1 else jnp.concatenate(parts, axis=1)
+
+
+def inverse_body(points, overlap, group, wx, wy, wn, picks, out_h, out_l, mat):
+    extent = points + overlap
+    block = LANES
+    window = wx.shape[1]
+    first_col = pl.program_id(0) * group
+    for g in range(group):
+        c = first_col + g
+        own = pl.ds(pl.multiple_of(c * points, LANES), points)
+        own_x, own_y, own_n = wx[:, own], wy[:, own], wn[:, own]
+        pick = picks[c]
+        pick_col = to_col(pick[0:1]).astype(jnp.int32)
+        got = [jnp.zeros((overlap, 1), F32) for _ in range(3)]
+        step = 512 if window % 512 == 0 else LANES
+        for start in range(0, window, step):
+            lane = lax.broadcasted_iota(jnp.int32, (overlap, step), 1) + start
+            hit = lane == pick_col
+            for m, ref in enumerate((wx, wy, wn)):
+                got[m] = got[m] + jnp.sum(
+                    jnp.where(hit, ref[:, start : start + step], 0.0), axis=1, keepdims=True
+                )
+        far_x, far_y, far_n = (to_row(v) for v in got)
+        row_x = jnp.concatenate([own_x, far_x + pick[1:2]], axis=1)
+        row_y = jnp.concatenate([own_y, far_y + pick[2:3]], axis=1)
+        row_n = jnp.concatenate([own_n, far_n], axis=1)
+        col_x, col_y = to_col(row_x), to_col(row_y)
+        for start in range(0, extent, block):
+            tile = kernel_of(
+                col_x[start : start + block] - row_x, col_y[start : start + block] - row_y
+            )
+            sub = lax.broadcasted_iota(jnp.int32, (block, extent), 0) + start
+            lane = lax.broadcasted_iota(jnp.int32, (block, extent), 1)
+            mat[g, start : start + block, :] = tile + jnp.where(sub == lane, row_n, 0.0)
+
+    identity = eye_mask(block).astype(F32)
+
+    def block_inverses(schurs):
+        low, high = NOISE_MIN, block + NOISE_MAX
+        rho = (high - low) / (high + low)
+        scale = 2.0 / (high + low)
+        factor = 2.0 / (2.0 - rho * rho)
+        found = [factor * scale * (2.0 * identity - scale * s) for s in schurs]
+        rho = rho * rho / (2.0 - rho * rho)
+        done = False
+        while not done:
+            done = rho < 1e-4
+            factor = 1.0 if done else 2.0 / (2.0 - rho * rho)
+            times = LATE if rho < 0.02 else EARLY
+            images = [times(s, x) for s, x in zip(schurs, found)]
+            found = [
+                times(factor * x, 2.0 * identity - y) for x, y in zip(found, images)
+            ]
+            rho = rho * rho / (2.0 - rho * rho)
+        return found
+
+    def stage(k, carry):
+        here = pl.ds(pl.multiple_of(k * block, block), block)
+        pivots = block_inverses([mat[g, here, here] for g in range(group)])
+        lane = lax.broadcasted_iota(jnp.int32, (block, extent), 1) - k * block
+        sub = lax.broadcasted_iota(jnp.int32, (block, extent), 0)
+        inside = (lane >= 0) & (lane < block)
+        for g in range(group):
+            row = jnp.where(inside, (lane == sub).astype(F32), mat[g, here, :])
+            new_row = UPDATE(pivots[g], row)
+            col = mat[g, :, here]
+            mat[g, :, here] = jnp.zeros_like(col)
+            for r in range(extent // block):
+                rows = slice(r * block, (r + 1) * block)
+                mat[g, rows, :] = mat[g, rows, :] - UPDATE(col[rows], new_row)
+            mat[g, here, :] = new_row
+        return carry
+
+    lax.fori_loop(0, extent // block, stage, 0)
+    for g in range(group):
+        out_h[g], out_l[g] = split(mat[g])
+
+
+def inverses(wx, wy, wn, picks, columns, points, overlap):
+    extent = points + overlap
+    group = 2 if columns % 2 == 0 else 1
+    whole = lambda a: pl.BlockSpec(a.shape, lambda i: (0,) * a.ndim)
+    out = pl.BlockSpec((group, extent, extent), lambda i: (i, 0, 0))
+    return pl.pallas_call(
+        lambda *refs: inverse_body(points, overlap, group, *refs),
+        grid=(columns // group,),
+        in_specs=[whole(wx), whole(wy), whole(wn), whole(picks)],
+        out_specs=[out, out],
+        out_shape=[jax.ShapeDtypeStruct((columns, extent, extent), BF16)] * 2,
+        scratch_shapes=[pltpu.VMEM((group, extent, extent), F32)],
+        compiler_params=params("arbitrary", mib=24),
+        name="inverse",
+    )(wx, wy, wn, picks)
+
+
+def operator_block(own_x, own_y, far_x, far_y, points, rows, cols, is_self):
+    tile = 128
+    height = (rows[1] - rows[0]) * points
+    width = (cols[1] - cols[0]) * points
+
+    def body(ox, oy, fx, fy, out_h, out_l):
+        first = pl.program_id(0) * tile
+        c = rows[0] + first // points
+        here = pl.ds(pl.multiple_of(rows[0] * points + first, LANES), tile)
+        col_x, col_y = to_col(ox[:, here]), to_col(oy[:, here])
+        for d in range(cols[0], cols[1]):
+            there = slice(d * points, (d + 1) * points)
+            value = kernel_of(
+                col_x - fx[:, there], col_y - (fy[:, there] + (d - c).astype(F32))
+            )
+            if is_self:
+                sub = lax.broadcasted_iota(jnp.int32, value.shape, 0) + first + rows[0] * points
+                lane = lax.broadcasted_iota(jnp.int32, value.shape, 1) + d * points
+                value = jnp.where(sub == lane, 0.0, value)
+            put = slice((d - cols[0]) * points, (d - cols[0] + 1) * points)
+            out_h[:, put], out_l[:, put] = split(value)
+
+    whole = pl.BlockSpec(own_x.shape, lambda i: (0, 0))
+    out = pl.BlockSpec((tile, width), lambda i: (i, 0))
+    return pl.pallas_call(
+        body,
+        grid=(height // tile,),
+        in_specs=[whole] * 4,
+        out_specs=[out, out],
+        out_shape=[jax.ShapeDtypeStruct((height, width), BF16)] * 2,
+        compiler_params=params("arbitrary"),
+        name="kern",
+    )(own_x, own_y, far_x, far_y)
+
+
+def multiply(blocks, vectors, base, tile=256):
+    count = len(blocks)
+    height, lanes = blocks[0][0].shape[0], vectors[0].shape[1]
+    base = base if isinstance(base, tuple) else (base,)
+
+    def body(*refs):
+        mats, vecs = refs[: 2 * count], refs[2 * count : 3 * count]
+        bases = refs[3 * count : 3 * count + len(base)]
+        out = refs[3 * count + len(base)]
+        packed = refs[3 * count + len(base) + 1 :]
+
+        @pl.when(pl.program_id(0) == 0)
+        def _():
+            for vec, pack in zip(vecs, packed):
+                pack[...] = pair_of(vec[...])
+
+        total = bases[0][...]
+        if len(bases) == 3:
+            total = total * bases[1][...] - BASIS_SHIFT * bases[2][...]
+        elif len(bases) == 2:
+            total = total * bases[1][...]
+        for k in range(count):
+            for mat in mats[2 * k : 2 * k + 2]:
+                total = total + folded(mm(mat[...], packed[k][...]))
+        out[...] = total
+
+    mats = [m for pair in blocks for m in pair]
+    tiled = lambda width: pl.BlockSpec((tile, width), lambda i: (i, 0))
+    return pl.pallas_call(
+        body,
+        grid=(height // tile,),
+        in_specs=[tiled(m.shape[1]) for m in mats]
+        + [pl.BlockSpec(v.shape, lambda i: (0, 0)) for v in vectors]
+        + [tiled(lanes)] * len(base),
+        out_specs=tiled(lanes),
+        out_shape=jax.ShapeDtypeStruct((height, lanes), F32),
+        scratch_shapes=[pltpu.VMEM((v.shape[0], 2 * lanes), BF16) for v in vectors],
+        compiler_params=params("arbitrary"),
+        name="multiply",
+    )(*mats, *vectors, *base)
+
+
+def gather_rows(selector, vector):
+    def body(sel, vec, *outs):
+        packed = pair_of(vec[...])
+        for k, out in enumerate(outs):
+            out[...] = folded(mm(sel[k], packed))
+
+    count, height, _ = selector.shape
+    shape = jax.ShapeDtypeStruct((height, vector.shape[1]), F32)
+    return pl.pallas_call(
+        body, out_shape=[shape] * count, compiler_params=params(), name="gather"
+    )(selector, vector)
+
+
+def solve(inv_h, inv_l, vector, borrowed, spread, points, overlap):
+    columns = inv_h.shape[0]
+    lanes = vector.shape[1]
+
+    def body(ih, il, vec, b0, b1, b2, spr, own, back):
+        for c in range(columns):
+            rows = slice(c * points, (c + 1) * points)
+            lent = slice(c * overlap, (c + 1) * overlap)
+            ext = jnp.concatenate([vec[rows, :], b0[lent, :] + b1[lent, :] + b2[lent, :]], axis=0)
+            packed = pair_of(ext)
+            found = folded(mm(ih[c], packed)) + folded(mm(il[c], packed))
+            own[rows, :] = found[:points]
+            back[lent, :] = found[points:]
+        own[...] = own[...] + folded(mm(spr[...], pair_of(back[...])))
+
+    return pl.pallas_call(
+        body,
+        out_shape=[
+            jax.ShapeDtypeStruct((columns * points, lanes), F32),
+            jax.ShapeDtypeStruct((columns * overlap, lanes), F32),
+        ],
+        compiler_params=params(),
+        name="solve",
+    )(inv_h, inv_l, vector, *borrowed, spread)
+
+
+def add_returned(spread_a, spread_b, part, back_a, back_b):
+    def body(sa, sb, base, ba, bb, out):
+        out[...] = (
+            base[...]
+            + folded(mm(sa[...], pair_of(ba[...])))
+            + folded(mm(sb[...], pair_of(bb[...])))
+        )
+
+    return pl.pallas_call(
+        body,
+        out_shape=jax.ShapeDtypeStruct(part.shape, F32),
+        compiler_params=params(),
+        name="returned",
+    )(spread_a, spread_b, part, back_a, back_b)
+
+
+def gram(pairs, arrays):
+    lanes = arrays[0].shape[1]
+
+    def body(*refs):
+        out = refs[-1]
+        for row, (a, b) in enumerate(pairs):
+            out[row : row + 1, :] = jnp.sum(refs[a][...] * refs[b][...], axis=0, keepdims=True)
+        if len(pairs) < 8:
+            out[len(pairs) :, :] = jnp.zeros((8 - len(pairs), lanes), F32)
+
+    return pl.pallas_call(
+        body,
+        out_shape=jax.ShapeDtypeStruct((8, lanes), F32),
+        compiler_params=params(),
+        name="gram",
+    )(*arrays)
+
+
+def coefficients(inner):
+    steps = ITERS
+    shift = BASIS_SHIFT
+    zero = jnp.zeros_like(inner[0][0])
+    one = jnp.ones_like(zero)
+
+    def image(d):
+        out = [zero] * (steps + 1)
+        for j in range(steps):
+            if j + 1 < steps:
+                out[j] = out[j] + shift * d[j]
+            out[j + 1] = out[j + 1] + d[j]
+        return out
+
+    def product(a, b):
+        total = zero
+        for i in range(len(a)):
+            if a[i] is zero:
+                continue
+            for j in range(len(b)):
+                if b[j] is not zero:
+                    total = total + a[i] * b[j] * inner[i][j]
+        return total
+
+    res = [one] + [zero] * steps
+    direction = [one] + [zero] * (steps - 1)
+    sol = [zero] * steps
+    now = product(res[:steps], res[:steps])
+    for k in range(steps):
+        applied = image(direction)
+        size = now / product(applied, direction)
+        sol = [s + size * d for s, d in zip(sol, direction)]
+        res = [r - size * a for r, a in zip(res, applied)]
+        if k + 1 < steps:
+            later = product(res[:steps], res[:steps])
+            ratio = later / now
+            direction = [r + ratio * d for r, d in zip(res[:steps], direction)]
+            now = later
+    return sol, res
+
+
+def combine(totals, first, sols, ress, place, columns):
+    count = len(sols)
+    points, lanes = first.shape[0] // columns, first.shape[1]
+
+    def body(place_ref, tot, b, *refs):
+        vs, us = refs[:count], refs[count : 2 * count]
+        out = refs[2 * count]
+        sol, res = coefficients(unpack(lambda r: tot[r : r + 1, :]))
+        x = sol[0] * vs[0][...]
+        r = res[0] * b[...]
+        for k in range(count):
+            if k:
+                x = x + sol[k] * vs[k][...]
+            r = r + res[k + 1] * us[k][...]
+        out[0, 0] = x
+        out[0, 1] = r
+
+    part = pl.BlockSpec((points, lanes), lambda d, p: (p[d], 0))
+    return pl.pallas_call(
+        body,
+        grid_spec=pltpu.PrefetchScalarGridSpec(
+            num_scalar_prefetch=1,
+            grid=(columns,),
+            in_specs=[pl.BlockSpec(totals.shape, lambda d, p: (0, 0)), part] + [part] * (2 * count),
+            out_specs=pl.BlockSpec((1, 2, points, lanes), lambda d, p: (d, 0, 0, 0)),
+        ),
+        out_shape=jax.ShapeDtypeStruct((columns, 2, points, lanes), F32),
+        compiler_params=params("arbitrary"),
+        name="combine",
+    )(place, totals, first, *sols, *ress)
+
+
+def inner_rows():
+    early = [(i, j) for i in range(ITERS) for j in range(i, ITERS)]
+    late = [(ITERS, j) for j in range(ITERS)]
+    return early, late
+
+
+def unpack(value):
+    early, late = inner_rows()
+    table = [[None] * ITERS for _ in range(ITERS + 1)]
+    for row, (i, j) in enumerate(early):
+        table[i][j] = value(row)
+        table[j][i] = value(row)
+    for row, (i, j) in enumerate(late):
+        table[i][j] = value(8 + row)
+    return table
 
 
 def shifted(value, axis, by):
@@ -24,7 +456,7 @@
     return lax.ppermute(block, axis, route)
 
 
-def kernel_block(rows_pos, cols_pos):
+def plain_block(rows_pos, cols_pos):
     delta_x = rows_pos[0][:, None] - cols_pos[0][None, :]
     delta_y = rows_pos[1][:, None] - cols_pos[1][None, :]
     distance = jnp.sqrt(delta_x * delta_x + delta_y * delta_y)
@@ -64,7 +496,7 @@
     return lax.psum(column_sum(residue, precond), ("gx", "gy"))
 
 
-def shards(right_side, coords, noise, intersect):
+def plain_shards(right_side, coords, noise, intersect):
     points = right_side.shape[2]
     rhs_count = right_side.shape[3]
     intersect_len = intersect.shape[2]
@@ -107,7 +539,7 @@
     )
     ext_pos = jnp.concatenate([own_pos, ov_pos], axis=1)
     ext_noise = jnp.concatenate([own_noise, chosen[2]])
-    local_matrix = kernel_block(ext_pos, ext_pos) + jnp.diag(ext_noise)
+    local_matrix = plain_block(ext_pos, ext_pos) + jnp.diag(ext_noise)
     factor = jnp.linalg.cholesky(local_matrix)
     inv_factor = lax.linalg.triangular_solve(
         factor, jnp.eye(ext_len, dtype=jnp.float32), left_side=True, lower=True
@@ -168,7 +600,7 @@
         for operate_row_off in range(3):
             for operate_col_off in range(3):
                 accumulated = accumulated + jnp.dot(
-                    kernel_block(own_pos, positions[operate_row_off][operate_col_off]),
+                    plain_block(own_pos, positions[operate_row_off][operate_col_off]),
                     columns[operate_col_off][operate_row_off],
                     precision=HIGH,
                     preferred_element_type=jnp.float32,
@@ -184,6 +616,151 @@
     return (solution.reshape(1, 1, points, rhs_count), residual.reshape(1, 1, points, rhs_count))
 
 
+def ring_order(count):
+    if count % 8:
+        return list(range(count))
+    depth = count // 4
+    loop = [(z, 1) for z in range(depth)] + [(z, 0) for z in reversed(range(depth))]
+    order = []
+    for k in range(2 * depth):
+        z, y = loop[(k - depth // 2) % (2 * depth)]
+        order += [z * 4 + y * 2, z * 4 + y * 2 + 1]
+    return order
+
+
+def select(choices, index):
+    out = choices[0]
+    for k in range(1, len(choices)):
+        out = jnp.where(index == k, choices[k], out)
+    return out
+
+
+def shards(right_side, coords, noise, intersect):
+    points, rhs_count = right_side.shape[2:]
+    overlap = intersect.shape[2]
+    rows_x, columns = lax.axis_size("gx"), lax.axis_size("gy")
+    lanes = rhs_count // columns
+    both = ("gx", "gy")
+    j = lax.axis_index("gy")
+    order = ring_order(rows_x)
+    parity = lax.axis_index("gx") % 2
+    sign = (1 - 2 * parity).astype(F32)
+    swap_a, swap_b = [], []
+    for p in range(0, rows_x, 2):
+        for swap, a, b in (
+            (swap_a, order[p], order[p + 1]),
+            (swap_b, order[p + 1], order[(p + 2) % rows_x]),
+        ):
+            swap += [(a, b), (b, a)]
+    beside = lambda v: (lax.ppermute(v, "gx", swap_a), lax.ppermute(v, "gx", swap_b))
+
+    def dealt(k):
+        return [
+            (i * columns + c, order[i] * columns + (c + k) % columns)
+            for i in range(rows_x)
+            for c in range(columns)
+        ]
+
+    def collected(k):
+        return [
+            (order[i] * columns + h, i * columns + (h + k) % columns)
+            for i in range(rows_x)
+            for h in range(columns)
+        ]
+
+    own = jnp.concatenate(
+        [coords.reshape(2 * points), noise.reshape(points), intersect.reshape(overlap).astype(F32)]
+    )
+    got = [lax.ppermute(own, both, dealt(k)) for k in range(columns)]
+    geometry = jnp.stack([select(got, (j - c) % columns) for c in range(columns)])
+    rhs = right_side.reshape(points, rhs_count)
+    pieces = [rhs[:, h * lanes : (h + 1) * lanes] for h in range(columns)]
+    got = [
+        lax.ppermute(select(pieces, (j + k) % columns), both, dealt(k)) for k in range(columns)
+    ]
+    start = jnp.concatenate([select(got, (j - c) % columns) for c in range(columns)], axis=0)
+    geo_a, geo_b = beside(geometry)
+    geos = [geometry, geo_a, geo_b]
+    offsets = [jnp.zeros((), F32), sign, -sign]
+    flat = lambda g, k: g[:, k * points : (k + 1) * points].reshape(1, columns * points)
+    xs, ys, ns = ([flat(g, k) for g in geos] for k in range(3))
+    wx, wy, wn = (jnp.concatenate(v, axis=1) for v in (xs, ys, ns))
+
+    def decode(g):
+        ids = g[:, 3 * points :].astype(jnp.int32)
+        slot = ids // points
+        return slot // 3 - 1, slot % 3 - 1, ids % points
+
+    col_index = jnp.arange(columns, dtype=jnp.int32)[:, None]
+    row_off, col_off, row_in = decode(geometry)
+    side = jnp.where(row_off == 0, 0, jnp.where(row_off.astype(F32) == sign, 1, 2))
+    local = side * (columns * points) + (col_index + col_off) * points + row_in
+    picks = jnp.stack([v.astype(F32) for v in (local, row_off, col_off)], axis=1)
+    wanted = []
+    for g, off in zip(geos, offsets):
+        row_off, col_off, row_in = decode(g)
+        mine = row_off.astype(F32) == -off
+        wanted.append(jnp.where(mine, (col_index + col_off) * points + row_in, -1).reshape(-1))
+    wanted = jnp.stack(wanted)
+    at = jnp.arange(columns * points, dtype=jnp.int32)
+    selector = (wanted[:, :, None] == at).astype(BF16)
+    spread = (wanted[:, None, :] == at[:, None]).astype(BF16)
+
+    inv_h, inv_l = inverses(wx, wy, wn, picks, columns, points, overlap)
+    whole = (0, columns)
+    blocks = [
+        operator_block(xs[0], ys[0], xs[t] + offsets[t], ys[t], points, whole, whole, t == 0)
+        for t in range(3)
+    ]
+    scale = jnp.broadcast_to(
+        1.0 + geometry[:, 2 * points : 3 * points].reshape(columns * points, 1),
+        (columns * points, lanes),
+    )
+
+    def precondition(vector):
+        lent, to_a, to_b = gather_rows(selector, vector)
+        from_a = lax.ppermute(to_a, "gx", swap_a)
+        from_b = lax.ppermute(to_b, "gx", swap_b)
+        part, back = solve(
+            inv_h, inv_l, vector, (lent, from_a, from_b), spread[0], points, overlap
+        )
+        back_a, back_b = beside(back)
+        return add_returned(spread[1], spread[2], part, back_a, back_b)
+
+    def operate(vector, before, last):
+        near_a, near_b = beside(vector)
+        base = (vector, scale) + (() if last else (before,))
+        part = multiply(blocks[:2], [vector, near_a], base)
+        return multiply([blocks[2]], [near_b], part)
+
+    basis, images = [start], []
+    for k in range(ITERS):
+        images.append(precondition(basis[k]))
+        basis.append(operate(images[k], basis[k], k + 1 == ITERS))
+
+    early, late = inner_rows()
+    first = gram([(i, ITERS + c) for i, c in early], basis[:ITERS] + images)
+    second = gram([(0, 1 + c) for _, c in late], [basis[ITERS]] + images)
+    totals = jnp.concatenate([first, second], axis=0)
+
+    def exchanged(value, distance):
+        return lax.ppermute(value, "gx", [(g, g ^ distance) for g in range(rows_x)])
+
+    bits = [1 << b for b in range(rows_x.bit_length() - 1)]
+    for step in [bits[:1], bits[1:2]] + [bits[k : k + 2] for k in range(2, len(bits), 2)]:
+        routes = step if len(step) < 2 else [step[0], step[1], step[0] ^ step[1]]
+        totals = totals + sum(exchanged(totals, r) for r in routes)
+
+    turn = (j + jnp.arange(columns, dtype=jnp.int32)) % columns
+    ready = combine(totals, start, images, basis[1:], turn, columns)
+    sent = [lax.ppermute(ready[k], both, collected(k)) for k in range(columns)]
+    outs = []
+    for part in range(2):
+        pieces = [select([s[part] for s in sent], (j - h) % columns) for h in range(columns)]
+        outs.append(jnp.concatenate(pieces, axis=1).reshape(1, 1, points, rhs_count))
+    return tuple(outs)
+
+
 def solution(mesh):
     placed = (
         P("gx", "gy", None, None),
@@ -191,8 +768,10 @@
         P("gx", "gy", None),
         P("gx", "gy", None),
     )
+    rows_x, columns = mesh.shape["gx"], mesh.shape["gy"]
+    paired = columns == 2 and rows_x >= 4 and rows_x & (rows_x - 1) == 0
     return jax.shard_map(
-        shards,
+        shards if paired else plain_shards,
         mesh=mesh,
         in_specs=placed,
         out_specs=(P("gx", "gy", None, None), P("gx", "gy", None, None)),

time: 756 us -> 172 us (0.23)
  blocking collectives: 201 us -> 0 us
  other arithmetic: 168 us -> 5.4 us
  waiting for transfers between devices: 161 us -> 58.6 us
  matrix products: 94.8 us -> 0 us
  Pallas kernels: 0 us -> 68.9 us
  starting transfers between devices: 96.9 us -> 37 us
  local copies, waits for them, and re-layouts: 22.5 us -> 1.12 us
    psum x5 -> x0, blocking collectives: 201 us -> none  [the longest x3 115 us: residual_dot(): return lax.psum(column_sum(residue, precond), ('gx', 'gy'))]
    another operation x35 -> x3, other arithmetic: 156 us -> 0.04 us  [the longest x1 0.02 us: shards(): jnp.stack([select(got, (j - c) % columns) for c in range(columns)])]
    ppermute x44 -> x31, waiting for transfers between devices: 161 us -> 58.6 us  [the longest x7 23.8 us: shards(): lax.ppermute(v, 'gx', swap_b)]
    dot_general x49 -> x0, matrix products: 76.7 us -> none  [the longest x27 52.9 us: shards(): jnp.dot(kernel_block(own_pos, positions[operate_row_off][operate_col_off]...]
    pallas_call x0 -> x22, Pallas kernels: none -> 68.9 us  [the longest x1 31.5 us: inverses(): pl.pallas_call(lambda *refs: inverse_body(points, overlap, group, *refs),...]
    ppermute x44 -> x31, starting transfers between devices: 96.9 us -> 37 us  [the longest x2 7.33 us: shards(): got = [lax.ppermute(own, both, dealt(k)) for k in range(columns)]]
    another operation x17 -> x0, matrix products: 18.1 us -> none  [the longest x9 10.5 us: shards(): lax.linalg.triangular_solve(factor, jnp.eye(ext_len, dtype=jnp.float32),...]
    another operation x24 -> x2, local copies, waits for them, and re-layouts: 17.6 us -> 0.01 us  [shards(): jnp.stack([select(got, (j - c) % columns) for c in range(columns)])]
  transfers between devices with their start and end apart: 44 -> 31, of which waited for: 24 -> 19; matrix products, arithmetic and copies ran while one was open for 33% -> 2% of each run, Pallas kernels for 0% -> 31%
where the time goes in v1:
time: 172 us
  Pallas kernels  68.9 us (40%)
  waiting for transfers between devices  58.6 us (34%)
  starting transfers between devices  37 us (22%)
  other arithmetic  5.4 us (3%)
    pallas_call x1, Pallas kernels, inverses(): pl.pallas_call(lambda *refs: inverse_body(points, overlap, group, *refs),...  31.5 us
    ppermute x7, waiting for transfers between devices, shards(): lax.ppermute(v, 'gx', swap_b)  23.8 us
    ppermute x2, waiting for transfers between devices, shards(): sent = [lax.ppermute(ready[k], both, collected(k)) for k in range(columns)]  18.9 us
    pallas_call x6, Pallas kernels, multiply(): pl.pallas_call(body, grid=(height // tile,), in_specs=[tiled(m.shape[1])...  14.8 us
    pallas_call x3, Pallas kernels, operator_block(): pl.pallas_call(body, grid=(height // tile,), in_specs=[whole] * 4, out_sp...  12.7 us
    ppermute x2, starting transfers between devices, shards(): got = [lax.ppermute(own, both, dealt(k)) for k in range(columns)]  7.33 us
    ppermute x3, waiting for transfers between devices, precondition(): from_b = lax.ppermute(to_b, 'gx', swap_b)  6.29 us
    ppermute x7, starting transfers between devices, shards(): lax.ppermute(v, 'gx', swap_b)  6.22 us
  transfers between devices with their start and end apart: 31, of which 19 were waited for; matrix products, arithmetic and copies ran while one was open for 2% of the time, Pallas kernels for 31%

profile of v1, /device:TPU:0, one launch (start us, length us, event | category | flops | bytes accessed | tf_op | source)
XLA Modules:
  0.0 172.2 jit_solution(18198418736270954254)
XLA Ops:
  2.7 4.9 %collective-permute-start.3 = (f32[1664]{0:T(1024)S(1)}, f32[1664]{0:T(1024)S(1)}, u32[]{:S(2)}, u32[]{:S(2)}) collective-permute-start(f32[1664]{0:T(1024)S(1)} %pad_maximum_fusion.5), channel_id=1, source_target_pairs={{0,8},{1,9},{2,10},{3,11},{4,0},{5,1},{6,2},{7,3},{8,4},{9,5},{10,... | collective-permute-start | bytes 19976 | tf_op jit(solution)/shard_map/ppermute | solution.py:674
  7.6 2.4 %collective-permute-start.2 = (f32[1664]{0:T(1024)S(1)}, f32[1664]{0:T(1024)S(1)}, u32[]{:S(2)}, u32[]{:S(2)}) collective-permute-start(f32[1664]{0:T(1024)S(1)} %pad_maximum_fusion.5), channel_id=1, source_target_pairs={{0,9},{1,8},{2,11},{3,10},{4,1},{5,0},{6,3},{7,2},{8,5},{9,4},{10,... | collective-permute-start | bytes 19976 | tf_op jit(solution)/shard_map/ppermute | solution.py:674
  10.0 1.1 slice_select_fusion
  11.1 2.4 %collective-permute-start.1 = (f32[512,128]{1,0:T(8,128)S(1)}, f32[512,128]{1,0:T(8,128)S(1)}, u32[]{:S(2)}, u32[]{:S(2)}) collective-permute-start(f32[512,128]{1,0:T(8,128)S(1)} %get-tuple-element.65), channel_id=1, source_target_pairs={{0,8},{1,9},{2,10},{3,11},{4,0},{5,1},{6,2},{7,3},{8,4},{9,5},{10,... | collective-permute-start | bytes 786440 | tf_op jit(solution)/shard_map/ppermute | solution.py:679
  13.5 1.6 collective-permute-start
  15.3 1.5 collective-permute-start.4
  16.9 7.8 %collective-permute-done.4 = f32[2,1664]{1,0:T(2,128)S(1)} collective-permute-done((f32[2,1664]{1,0:T(2,128)S(1)}, f32[2,1664]{1,0:T(2,128)S(1)}, u32[]{:S(2)}, u32[]{:S(2)}) %collective-permute-start.4) | collective-permute-done | bytes 13344 | tf_op jit(solution)/shard_map/ppermute | solution.py:655
  26.8 1.3 collective-permute-start.6
  28.2 31.5 %inverse.1 = (bf16[2,640,640]{2,1,0:T(8,128)(2,1)S(1)}, bf16[2,640,640]{2,1,0:T(8,128)(2,1)S(1)}) custom-call(f32[1,3072]{1,0:T(1,128)S(1)} %get-tuple-element.80.refs_0_, f32[1,3072]{1,0:T(1,128)S(1)} %get-tuple-element.81.refs_1_, f32[1,3072]{1,0:T(1,128)S(1)} %pad_maximum_fusion.4.refs_2_, f32[2,3,128]{2,1,0:T(4,128)S(1)} %pad_maximum_fusion.7.refs_3_), custom_call_target="tpu_custom_call" | custom-call | tf_op jit(solution)/shard_map/inverse/pallas_call | solution.py:196
  59.7 1.7 %solve.3 = (f32[1024,128]{1,0:T(8,128)S(1)}, f32[256,128]{1,0:T(8,128)S(1)}) custom-call(bf16[2,640,640]{2,1,0:T(8,128)(2,1)S(1)} %get-tuple-element.27.ih, bf16[2,640,640]{2,1,0:T(8,128)(2,1)S(1)} %get-tuple-element.28.il, f32[1024,128]{1,0:T(8,128)S(1)} %pad_maximum_fusion.vec.refs_8_.refs_0_.b, f32[256,128]{1,0:T(8,128)S(1)} %get-tuple-element.29.b0, ...), custom_call_target="tpu_custom_call" | custom-call | tf_op jit(solution)/shard_map/solve/pallas_call | solution.py:313
  61.5 1.8 %collective-permute-start.9 = (f32[256,128]{1,0:T(8,128)S(1)}, f32[256,128]{1,0:T(8,128)S(1)}, u32[]{:S(2)}, u32[]{:S(2)}) collective-permute-start(f32[256,128]{1,0:T(8,128)S(1)} %get-tuple-element.33), channel_id=1, source_target_pairs={{10,0},{0,10},{2,4},{4,2},{6,12},{12,6},{14,20},{20,14},{22,28},{2... | collective-permute-start | bytes 393224 | tf_op jit(solution)/shard_map/ppermute | solution.py:655
  63.3 2.6 %collective-permute-done.9.bb = f32[256,128]{1,0:T(8,128)S(1)} collective-permute-done((f32[256,128]{1,0:T(8,128)S(1)}, f32[256,128]{1,0:T(8,128)S(1)}, u32[]{:S(2)}, u32[]{:S(2)}) %collective-permute-start.9) | collective-permute-done | bytes 131104 | tf_op jit(solution)/shard_map/ppermute | solution.py:655
  66.4 1.8 %collective-permute-start.11 = (f32[1024,128]{1,0:T(8,128)S(1)}, f32[1024,128]{1,0:T(8,128)S(1)}, u32[]{:S(2)}, u32[]{:S(2)}) collective-permute-start(f32[1024,128]{1,0:T(8,128)S(1)} %returned.3.refs_4_.refs_6_.refs_3_.refs_1_.refs_0_), channel_id=1, source_target_pairs={{8,10},{10,8},{0,2},{2,0},{4,6},{6,4},{12,14},{14,12},{20,22},{22,... | collective-permute-start | bytes 1572872 | tf_op jit(solution)/shard_map/ppermute | solution.py:655
  68.2 1.4 collective-permute-start.10
  69.6 4.5 %kern.4 = (bf16[1024,1024]{1,0:T(8,128)(2,1)S(1)}, bf16[1024,1024]{1,0:T(8,128)(2,1)S(1)}) custom-call(f32[1,1024]{1,0:T(1,128)S(1)} %bitcast.77, f32[1,1024]{1,0:T(1,128)S(1)} %bitcast.82, f32[1,1024]{1,0:T(1,128)S(1)} %bitcast.78, f32[1,1024]{1,0:T(1,128)S(1)} %bitcast.83), custom_call_target="tpu_custom_call" | custom-call | tf_op jit(solution)/shard_map/kern/pallas_call | solution.py:232
  74.0 4.1 %kern.5 = (bf16[1024,1024]{1,0:T(8,128)(2,1)S(1)}, bf16[1024,1024]{1,0:T(8,128)(2,1)S(1)}) custom-call(f32[1,1024]{1,0:T(1,128)S(1)} %bitcast.79, f32[1,1024]{1,0:T(1,128)S(1)} %bitcast.84, f32[1,1024]{1,0:T(1,128)S(1)} %broadcast_add_fusion.fx, f32[1,1024]{1,0:T(1,128)S(1)} %bitcast.87), custom_call_target="tpu_custom_call" | custom-call | tf_op jit(solution)/shard_map/kern/pallas_call | solution.py:232
  78.2 4.1 %kern.3 = (bf16[1024,1024]{1,0:T(8,128)(2,1)S(1)}, bf16[1024,1024]{1,0:T(8,128)(2,1)S(1)}) custom-call(f32[1,1024]{1,0:T(1,128)S(1)} %bitcast.80, f32[1,1024]{1,0:T(1,128)S(1)} %bitcast.85, f32[1,1024]{1,0:T(1,128)S(1)} %broadcast_add_fusion.1.fx, f32[1,1024]{1,0:T(1,128)S(1)} %bitcast.89), custom_call_target="tpu_custom_call" | custom-call | tf_op jit(solution)/shard_map/kern/pallas_call | solution.py:232
  82.5 3.1 %multiply.6.refs_3_ = f32[1024,128]{1,0:T(8,128)S(1)} custom-call(bf16[1024,1024]{1,0:T(8,128)(2,1)S(1)} %get-tuple-element.34.refs_0_, bf16[1024,1024]{1,0:T(8,128)(2,1)S(1)} %get-tuple-element.35.refs_1_, bf16[1024,1024]{1,0:T(8,128)(2,1)S(1)} %get-tuple-element.36.refs_2_, bf16[1024,1024]{1,0:T(8,128)(2,1)S(1)} %get-tuple-element.37.refs_3_, ...), custom_call_target="tpu_custom_call" | custom-call | tf_op jit(solution)/shard_map/multiply/pallas_call | solution.py:271
  85.6 1.9 %multiply.7.vec.refs_8_.refs_1_.refs_3_ = f32[1024,128]{1,0:T(8,128)S(1)} custom-call(bf16[1024,1024]{1,0:T(8,128)(2,1)S(1)} %get-tuple-element.25.refs_0_, bf16[1024,1024]{1,0:T(8,128)(2,1)S(1)} %get-tuple-element.26.refs_1_, f32[1024,128]{1,0:T(8,128)S(1)} %collective-permute-done.10.refs_2_, f32[1024,128]{1,0:T(8,128)S(1)} %multiply.6.refs_3_), custom_call_target="tpu_custom_call" | custom-call | tf_op jit(solution)/shard_map/multiply/pallas_call | solution.py:271
  88.6 0.9 collective-permute-done.12.b1
  89.5 3.1 %collective-permute-done.13.b2 = f32[256,128]{1,0:T(8,128)S(1)} collective-permute-done((f32[256,128]{1,0:T(8,128)S(1)}, f32[256,128]{1,0:T(8,128)S(1)}, u32[]{:S(2)}, u32[]{:S(2)}) %collective-permute-start.13) | collective-permute-done | bytes 131104 | tf_op jit(solution)/shard_map/ppermute | solution.py:723
  92.6 1.7 %solve.4 = (f32[1024,128]{1,0:T(8,128)S(1)}, f32[256,128]{1,0:T(8,128)S(1)}) custom-call(bf16[2,640,640]{2,1,0:T(8,128)(2,1)S(1)} %get-tuple-element.27.ih, bf16[2,640,640]{2,1,0:T(8,128)(2,1)S(1)} %get-tuple-element.28.il, f32[1024,128]{1,0:T(8,128)S(1)} %multiply.7.vec.refs_8_.refs_1_.refs_3_, f32[256,128]{1,0:T(8,128)S(1)} %get-tuple-element.38.b0, ...), custom_call_target="tpu_custom_call" | custom-call | tf_op jit(solution)/shard_map/solve/pallas_call | solution.py:313
  94.8 1.3 collective-permute-start.14
  96.2 2.7 %collective-permute-done.15.bb = f32[256,128]{1,0:T(8,128)S(1)} collective-permute-done((f32[256,128]{1,0:T(8,128)S(1)}, f32[256,128]{1,0:T(8,128)S(1)}, u32[]{:S(2)}, u32[]{:S(2)}) %collective-permute-start.15) | collective-permute-done | bytes 131104 | tf_op jit(solution)/shard_map/ppermute | solution.py:655
  100.1 1.2 collective-permute-done.17.refs_5_
  101.3 3.1 %multiply.8.refs_3_ = f32[1024,128]{1,0:T(8,128)S(1)} custom-call(bf16[1024,1024]{1,0:T(8,128)(2,1)S(1)} %get-tuple-element.34.refs_0_, bf16[1024,1024]{1,0:T(8,128)(2,1)S(1)} %get-tuple-element.35.refs_1_, bf16[1024,1024]{1,0:T(8,128)(2,1)S(1)} %get-tuple-element.36.refs_2_, bf16[1024,1024]{1,0:T(8,128)(2,1)S(1)} %get-tuple-element.37.refs_3_, ...), custom_call_target="tpu_custom_call" | custom-call | tf_op jit(solution)/shard_map/multiply/pallas_call | solution.py:271
  104.4 4.0 %collective-permute-done.16.refs_2_ = f32[1024,128]{1,0:T(8,128)S(1)} collective-permute-done((f32[1024,128]{1,0:T(8,128)S(1)}, f32[1024,128]{1,0:T(8,128)S(1)}, u32[]{:S(2)}, u32[]{:S(2)}) %collective-permute-start.16) | collective-permute-done | bytes 524320 | tf_op jit(solution)/shard_map/ppermute | solution.py:655
  108.4 1.9 %multiply.9.vec.refs_2_.refs_4_ = f32[1024,128]{1,0:T(8,128)S(1)} custom-call(bf16[1024,1024]{1,0:T(8,128)(2,1)S(1)} %get-tuple-element.25.refs_0_, bf16[1024,1024]{1,0:T(8,128)(2,1)S(1)} %get-tuple-element.26.refs_1_, f32[1024,128]{1,0:T(8,128)S(1)} %collective-permute-done.16.refs_2_, f32[1024,128]{1,0:T(8,128)S(1)} %multiply.8.refs_3_), custom_call_target="tpu_custom_call" | custom-call | tf_op jit(solution)/shard_map/multiply/pallas_call | solution.py:271
  111.4 0.9 collective-permute-done.18.b1
  112.3 3.2 %collective-permute-done.19.b2 = f32[256,128]{1,0:T(8,128)S(1)} collective-permute-done((f32[256,128]{1,0:T(8,128)S(1)}, f32[256,128]{1,0:T(8,128)S(1)}, u32[]{:S(2)}, u32[]{:S(2)}) %collective-permute-start.19) | collective-permute-done | bytes 131104 | tf_op jit(solution)/shard_map/ppermute | solution.py:723
  115.4 1.7 %solve.5 = (f32[1024,128]{1,0:T(8,128)S(1)}, f32[256,128]{1,0:T(8,128)S(1)}) custom-call(bf16[2,640,640]{2,1,0:T(8,128)(2,1)S(1)} %get-tuple-element.27.ih, bf16[2,640,640]{2,1,0:T(8,128)(2,1)S(1)} %get-tuple-element.28.il, f32[1024,128]{1,0:T(8,128)S(1)} %multiply.9.vec.refs_2_.refs_4_, f32[256,128]{1,0:T(8,128)S(1)} %get-tuple-element.43.b0, ...), custom_call_target="tpu_custom_call" | custom-call | tf_op jit(solution)/shard_map/solve/pallas_call | solution.py:313
  117.6 1.3 collective-permute-start.20
  118.9 2.7 %collective-permute-done.21.bb = f32[256,128]{1,0:T(8,128)S(1)} collective-permute-done((f32[256,128]{1,0:T(8,128)S(1)}, f32[256,128]{1,0:T(8,128)S(1)}, u32[]{:S(2)}, u32[]{:S(2)}) %collective-permute-start.21) | collective-permute-done | bytes 131104 | tf_op jit(solution)/shard_map/ppermute | solution.py:655
  124.1 3.1 %multiply.10.refs_3_ = f32[1024,128]{1,0:T(8,128)S(1)} custom-call(bf16[1024,1024]{1,0:T(8,128)(2,1)S(1)} %get-tuple-element.34.refs_0_, bf16[1024,1024]{1,0:T(8,128)(2,1)S(1)} %get-tuple-element.35.refs_1_, bf16[1024,1024]{1,0:T(8,128)(2,1)S(1)} %get-tuple-element.36.refs_2_, bf16[1024,1024]{1,0:T(8,128)(2,1)S(1)} %get-tuple-element.37.refs_3_, ...), custom_call_target="tpu_custom_call" | custom-call | tf_op jit(solution)/shard_map/multiply/pallas_call | solution.py:271
  127.1 4.0 %collective-permute-done.22.refs_2_ = f32[1024,128]{1,0:T(8,128)S(1)} collective-permute-done((f32[1024,128]{1,0:T(8,128)S(1)}, f32[1024,128]{1,0:T(8,128)S(1)}, u32[]{:S(2)}, u32[]{:S(2)}) %collective-permute-start.22) | collective-permute-done | bytes 524320 | tf_op jit(solution)/shard_map/ppermute | solution.py:655
  131.1 1.9 %multiply.11.refs_0_.refs_5_ = f32[1024,128]{1,0:T(8,128)S(1)} custom-call(bf16[1024,1024]{1,0:T(8,128)(2,1)S(1)} %get-tuple-element.25.refs_0_, bf16[1024,1024]{1,0:T(8,128)(2,1)S(1)} %get-tuple-element.26.refs_1_, f32[1024,128]{1,0:T(8,128)S(1)} %collective-permute-done.22.refs_2_, f32[1024,128]{1,0:T(8,128)S(1)} %multiply.10.refs_3_), custom_call_target="tpu_custom_call" | custom-call | tf_op jit(solution)/shard_map/multiply/pallas_call | solution.py:271
  133.4 1.0 collective-permute-done.24
  134.5 1.3 collective-permute-start.25
  135.8 2.3 %collective-permute-done.25 = f32[16,128]{1,0:T(8,128)S(1)} collective-permute-done((f32[16,128]{1,0:T(8,128)S(1)}, f32[16,128]{1,0:T(8,128)S(1)}, u32[]{:S(2)}, u32[]{:S(2)}) %collective-permute-start.25) | collective-permute-done | bytes 8224 | tf_op jit(solution)/shard_map/ppermute | solution.py:747
  138.2 2.1 %collective-permute-start.28 = (f32[16,128]{1,0:T(8,128)S(1)}, f32[16,128]{1,0:T(8,128)S(1)}, u32[]{:S(2)}, u32[]{:S(2)}) collective-permute-start(f32[16,128]{1,0:T(8,128)S(1)} %add.195), channel_id=1, source_target_pairs={{0,24},{2,26},{4,28},{6,30},{8,16},{10,18},{12,20},{14,22},{16,8},... | collective-permute-start | bytes 24584 | tf_op jit(solution)/shard_map/ppermute | solution.py:747
  140.3 2.3 %collective-permute-start.26 = (f32[16,128]{1,0:T(8,128)S(1)}, f32[16,128]{1,0:T(8,128)S(1)}, u32[]{:S(2)}, u32[]{:S(2)}) collective-permute-start(f32[16,128]{1,0:T(8,128)S(1)} %add.195), channel_id=1, source_target_pairs={{0,8},{2,10},{4,12},{6,14},{8,0},{10,2},{12,4},{14,6},{16,24},{18,... | collective-permute-start | bytes 24584 | tf_op jit(solution)/shard_map/ppermute | solution.py:747
  142.6 1.0 collective-permute-done.28
  143.6 1.2 collective-permute-done.27
  144.9 1.0 combine.1
  145.9 1.5 collective-permute-start.29
  147.4 4.2 %collective-permute-start.30 = (f32[2,512,128]{2,1,0:T(8,128)S(1)}, f32[2,512,128]{2,1,0:T(8,128)S(1)}, u32[]{:S(2)}, u32[]{:S(2)}) collective-permute-start(f32[2,512,128]{2,1,0:T(8,128)S(1)} %get-tuple-element.62), channel_id=1, source_target_pairs={{8,0},{9,1},{10,2},{11,3},{0,4},{1,5},{2,6},{3,7},{4,8},{5,9},{6,1... | collective-permute-start | bytes 1572872 | tf_op jit(solution)/shard_map/ppermute | solution.py:756
  151.6 16.2 %collective-permute-done.29 = f32[2,512,128]{2,1,0:T(8,128)S(1)} collective-permute-done((f32[2,512,128]{2,1,0:T(8,128)S(1)}, f32[2,512,128]{2,1,0:T(8,128)S(1)}, u32[]{:S(2)}, u32[]{:S(2)}) %collective-permute-start.29) | collective-permute-done | bytes 524320 | tf_op jit(solution)/shard_map/ppermute | solution.py:756
  167.8 2.6 %collective-permute-done.30 = f32[2,512,128]{2,1,0:T(8,128)S(1)} collective-permute-done((f32[2,512,128]{2,1,0:T(8,128)S(1)}, f32[2,512,128]{2,1,0:T(8,128)S(1)}, u32[]{:S(2)}, u32[]{:S(2)}) %collective-permute-start.30) | collective-permute-done | bytes 524320 | tf_op jit(solution)/shard_map/ppermute | solution.py:756
  (82 shorter events, 14.1 us)
Async XLA Ops:
  2.7 12.4 %collective-permute-start.3 = (f32[1664]{0:T(1024)S(1)}, f32[1664]{0:T(1024)S(1)}, u32[]{:S(2)}, u32[]{:S(2)}) collective-permute-start(f32[1664]{0:T(1024)S(1)} %pad_maximum_fusion.5), channel_id=1, source_target_pairs={{0,8},{1,9},{2,10},{3,11},{4,0},{5,1},{6,2},{7,3},{8,4},{9,5},{10,... | collective-permute-start | bytes 19976 | tf_op jit(solution)/shard_map/ppermute | solution.py:674
  7.6 7.5 %collective-permute-start.2 = (f32[1664]{0:T(1024)S(1)}, f32[1664]{0:T(1024)S(1)}, u32[]{:S(2)}, u32[]{:S(2)}) collective-permute-start(f32[1664]{0:T(1024)S(1)} %pad_maximum_fusion.5), channel_id=1, source_target_pairs={{0,9},{1,8},{2,11},{3,10},{4,1},{5,0},{6,3},{7,2},{8,5},{9,4},{10,... | collective-permute-start | bytes 19976 | tf_op jit(solution)/shard_map/ppermute | solution.py:674
  11.1 15.0 %collective-permute-start.1 = (f32[512,128]{1,0:T(8,128)S(1)}, f32[512,128]{1,0:T(8,128)S(1)}, u32[]{:S(2)}, u32[]{:S(2)}) collective-permute-start(f32[512,128]{1,0:T(8,128)S(1)} %get-tuple-element.65), channel_id=1, source_target_pairs={{0,8},{1,9},{2,10},{3,11},{4,0},{5,1},{6,2},{7,3},{8,4},{9,5},{10,... | collective-permute-start | bytes 786440 | tf_op jit(solution)/shard_map/ppermute | solution.py:679
  13.5 12.6 %collective-permute-start = (f32[512,128]{1,0:T(8,128)S(1)}, f32[512,128]{1,0:T(8,128)S(1)}, u32[]{:S(2)}, u32[]{:S(2)}) collective-permute-start(f32[512,128]{1,0:T(8,128)S(1)} %get-tuple-element.66), channel_id=1, source_target_pairs={{0,9},{1,8},{2,11},{3,10},{4,1},{5,0},{6,3},{7,2},{8,5},{9,4},{10,... | collective-permute-start | bytes 786440 | tf_op jit(solution)/shard_map/ppermute | solution.py:679
  15.2 1.7 collective-permute-start.5
  15.3 9.4 %collective-permute-start.4 = (f32[2,1664]{1,0:T(2,128)S(1)}, f32[2,1664]{1,0:T(2,128)S(1)}, u32[]{:S(2)}, u32[]{:S(2)}) collective-permute-start(f32[2,1664]{1,0:T(2,128)S(1)} %pad_maximum_fusion.1), channel_id=1, source_target_pairs={{10,0},{0,10},{2,4},{4,2},{6,12},{12,6},{14,20},{20,14},{22,28},{2... | collective-permute-start | bytes 39944 | tf_op jit(solution)/shard_map/ppermute | solution.py:655
  26.8 33.0 %collective-permute-start.6 = (f32[256,128]{1,0:T(8,128)S(1)}, f32[256,128]{1,0:T(8,128)S(1)}, u32[]{:S(2)}, u32[]{:S(2)}) collective-permute-start(f32[256,128]{1,0:T(8,128)S(1)} %get-tuple-element.30), channel_id=1, source_target_pairs={{8,10},{10,8},{0,2},{2,0},{4,6},{6,4},{12,14},{14,12},{20,22},{22,... | collective-permute-start | bytes 393224 | tf_op jit(solution)/shard_map/ppermute | solution.py:722
  28.1 31.6 %collective-permute-start.7 = (f32[256,128]{1,0:T(8,128)S(1)}, f32[256,128]{1,0:T(8,128)S(1)}, u32[]{:S(2)}, u32[]{:S(2)}) collective-permute-start(f32[256,128]{1,0:T(8,128)S(1)} %get-tuple-element.31), channel_id=1, source_target_pairs={{10,0},{0,10},{2,4},{4,2},{6,12},{12,6},{14,20},{20,14},{22,28},{2... | collective-permute-start | bytes 393224 | tf_op jit(solution)/shard_map/ppermute | solution.py:723
  61.5 4.5 %collective-permute-start.9 = (f32[256,128]{1,0:T(8,128)S(1)}, f32[256,128]{1,0:T(8,128)S(1)}, u32[]{:S(2)}, u32[]{:S(2)}) collective-permute-start(f32[256,128]{1,0:T(8,128)S(1)} %get-tuple-element.33), channel_id=1, source_target_pairs={{10,0},{0,10},{2,4},{4,2},{6,12},{12,6},{14,20},{20,14},{22,28},{2... | collective-permute-start | bytes 393224 | tf_op jit(solution)/shard_map/ppermute | solution.py:655
  63.2 2.7 %collective-permute-start.8 = (f32[256,128]{1,0:T(8,128)S(1)}, f32[256,128]{1,0:T(8,128)S(1)}, u32[]{:S(2)}, u32[]{:S(2)}) collective-permute-start(f32[256,128]{1,0:T(8,128)S(1)} %get-tuple-element.33), channel_id=1, source_target_pairs={{8,10},{10,8},{0,2},{2,0},{4,6},{6,4},{12,14},{14,12},{20,22},{22,... | collective-permute-start | bytes 393224 | tf_op jit(solution)/shard_map/ppermute | solution.py:655
  66.4 15.9 %collective-permute-start.11 = (f32[1024,128]{1,0:T(8,128)S(1)}, f32[1024,128]{1,0:T(8,128)S(1)}, u32[]{:S(2)}, u32[]{:S(2)}) collective-permute-start(f32[1024,128]{1,0:T(8,128)S(1)} %returned.3.refs_4_.refs_6_.refs_3_.refs_1_.refs_0_), channel_id=1, source_target_pairs={{8,10},{10,8},{0,2},{2,0},{4,6},{6,4},{12,14},{14,12},{20,22},{22,... | collective-permute-start | bytes 1572872 | tf_op jit(solution)/shard_map/ppermute | solution.py:655
  68.2 17.5 %collective-permute-start.10 = (f32[1024,128]{1,0:T(8,128)S(1)}, f32[1024,128]{1,0:T(8,128)S(1)}, u32[]{:S(2)}, u32[]{:S(2)}) collective-permute-start(f32[1024,128]{1,0:T(8,128)S(1)} %returned.3.refs_4_.refs_6_.refs_3_.refs_1_.refs_0_), channel_id=1, source_target_pairs={{10,0},{0,10},{2,4},{4,2},{6,12},{12,6},{14,20},{20,14},{22,28},{2... | collective-permute-start | bytes 1572872 | tf_op jit(solution)/shard_map/ppermute | solution.py:655
  88.1 1.4 collective-permute-start.12
  88.2 4.5 %collective-permute-start.13 = (f32[256,128]{1,0:T(8,128)S(1)}, f32[256,128]{1,0:T(8,128)S(1)}, u32[]{:S(2)}, u32[]{:S(2)}) collective-permute-start(f32[256,128]{1,0:T(8,128)S(1)} %get-tuple-element.40), channel_id=1, source_target_pairs={{10,0},{0,10},{2,4},{4,2},{6,12},{12,6},{14,20},{20,14},{22,28},{2... | collective-permute-start | bytes 393224 | tf_op jit(solution)/shard_map/ppermute | solution.py:723
  94.4 4.5 %collective-permute-start.15 = (f32[256,128]{1,0:T(8,128)S(1)}, f32[256,128]{1,0:T(8,128)S(1)}, u32[]{:S(2)}, u32[]{:S(2)}) collective-permute-start(f32[256,128]{1,0:T(8,128)S(1)} %get-tuple-element.42), channel_id=1, source_target_pairs={{10,0},{0,10},{2,4},{4,2},{6,12},{12,6},{14,20},{20,14},{22,28},{2... | collective-permute-start | bytes 393224 | tf_op jit(solution)/shard_map/ppermute | solution.py:655
  94.8 4.0 %collective-permute-start.14 = (f32[256,128]{1,0:T(8,128)S(1)}, f32[256,128]{1,0:T(8,128)S(1)}, u32[]{:S(2)}, u32[]{:S(2)}) collective-permute-start(f32[256,128]{1,0:T(8,128)S(1)} %get-tuple-element.42), channel_id=1, source_target_pairs={{8,10},{10,8},{0,2},{2,0},{4,6},{6,4},{12,14},{14,12},{20,22},{22,... | collective-permute-start | bytes 393224 | tf_op jit(solution)/shard_map/ppermute | solution.py:655
  99.3 2.0 %collective-permute-start.17 = (f32[1024,128]{1,0:T(8,128)S(1)}, f32[1024,128]{1,0:T(8,128)S(1)}, u32[]{:S(2)}, u32[]{:S(2)}) collective-permute-start(f32[1024,128]{1,0:T(8,128)S(1)} %returned.4.refs_4_.refs_6_.refs_2_.refs_1_), channel_id=1, source_target_pairs={{8,10},{10,8},{0,2},{2,0},{4,6},{6,4},{12,14},{14,12},{20,22},{22,... | collective-permute-start | bytes 1572872 | tf_op jit(solution)/shard_map/ppermute | solution.py:655
  99.8 8.6 %collective-permute-start.16 = (f32[1024,128]{1,0:T(8,128)S(1)}, f32[1024,128]{1,0:T(8,128)S(1)}, u32[]{:S(2)}, u32[]{:S(2)}) collective-permute-start(f32[1024,128]{1,0:T(8,128)S(1)} %returned.4.refs_4_.refs_6_.refs_2_.refs_1_), channel_id=1, source_target_pairs={{10,0},{0,10},{2,4},{4,2},{6,12},{12,6},{14,20},{20,14},{22,28},{2... | collective-permute-start | bytes 1572872 | tf_op jit(solution)/shard_map/ppermute | solution.py:655
  110.9 1.4 collective-permute-start.18
  111.0 4.4 %collective-permute-start.19 = (f32[256,128]{1,0:T(8,128)S(1)}, f32[256,128]{1,0:T(8,128)S(1)}, u32[]{:S(2)}, u32[]{:S(2)}) collective-permute-start(f32[256,128]{1,0:T(8,128)S(1)} %get-tuple-element.45), channel_id=1, source_target_pairs={{10,0},{0,10},{2,4},{4,2},{6,12},{12,6},{14,20},{20,14},{22,28},{2... | collective-permute-start | bytes 393224 | tf_op jit(solution)/shard_map/ppermute | solution.py:723
  117.2 4.5 %collective-permute-start.21 = (f32[256,128]{1,0:T(8,128)S(1)}, f32[256,128]{1,0:T(8,128)S(1)}, u32[]{:S(2)}, u32[]{:S(2)}) collective-permute-start(f32[256,128]{1,0:T(8,128)S(1)} %get-tuple-element.47), channel_id=1, source_target_pairs={{10,0},{0,10},{2,4},{4,2},{6,12},{12,6},{14,20},{20,14},{22,28},{2... | collective-permute-start | bytes 393224 | tf_op jit(solution)/shard_map/ppermute | solution.py:655
  117.6 4.1 %collective-permute-start.20 = (f32[256,128]{1,0:T(8,128)S(1)}, f32[256,128]{1,0:T(8,128)S(1)}, u32[]{:S(2)}, u32[]{:S(2)}) collective-permute-start(f32[256,128]{1,0:T(8,128)S(1)} %get-tuple-element.47), channel_id=1, source_target_pairs={{8,10},{10,8},{0,2},{2,0},{4,6},{6,4},{12,14},{14,12},{20,22},{22,... | collective-permute-start | bytes 393224 | tf_op jit(solution)/shard_map/ppermute | solution.py:655
  122.1 2.0 %collective-permute-start.23 = (f32[1024,128]{1,0:T(8,128)S(1)}, f32[1024,128]{1,0:T(8,128)S(1)}, u32[]{:S(2)}, u32[]{:S(2)}) collective-permute-start(f32[1024,128]{1,0:T(8,128)S(1)} %returned.5.refs_5_.refs_4_.refs_6_.refs_3_.refs_2_), channel_id=1, source_target_pairs={{8,10},{10,8},{0,2},{2,0},{4,6},{6,4},{12,14},{14,12},{20,22},{22,... | collective-permute-start | bytes 1572872 | tf_op jit(solution)/shard_map/ppermute | solution.py:655
  122.5 8.6 %collective-permute-start.22 = (f32[1024,128]{1,0:T(8,128)S(1)}, f32[1024,128]{1,0:T(8,128)S(1)}, u32[]{:S(2)}, u32[]{:S(2)}) collective-permute-start(f32[1024,128]{1,0:T(8,128)S(1)} %returned.5.refs_5_.refs_4_.refs_6_.refs_3_.refs_2_), channel_id=1, source_target_pairs={{10,0},{0,10},{2,4},{4,2},{6,12},{12,6},{14,20},{20,14},{22,28},{2... | collective-permute-start | bytes 1572872 | tf_op jit(solution)/shard_map/ppermute | solution.py:655
  133.3 1.2 collective-permute-start.24
  134.5 3.7 %collective-permute-start.25 = (f32[16,128]{1,0:T(8,128)S(1)}, f32[16,128]{1,0:T(8,128)S(1)}, u32[]{:S(2)}, u32[]{:S(2)}) collective-permute-start(f32[16,128]{1,0:T(8,128)S(1)} %fusion.21), channel_id=1, source_target_pairs={{0,4},{2,6},{4,0},{6,2},{8,12},{10,14},{12,8},{14,10},{16,20},{18,... | collective-permute-start | bytes 24584 | tf_op jit(solution)/shard_map/ppermute | solution.py:747
  138.2 5.4 %collective-permute-start.28 = (f32[16,128]{1,0:T(8,128)S(1)}, f32[16,128]{1,0:T(8,128)S(1)}, u32[]{:S(2)}, u32[]{:S(2)}) collective-permute-start(f32[16,128]{1,0:T(8,128)S(1)} %add.195), channel_id=1, source_target_pairs={{0,24},{2,26},{4,28},{6,30},{8,16},{10,18},{12,20},{14,22},{16,8},... | collective-permute-start | bytes 24584 | tf_op jit(solution)/shard_map/ppermute | solution.py:747
  140.3 4.5 %collective-permute-start.27 = (f32[16,128]{1,0:T(8,128)S(1)}, f32[16,128]{1,0:T(8,128)S(1)}, u32[]{:S(2)}, u32[]{:S(2)}) collective-permute-start(f32[16,128]{1,0:T(8,128)S(1)} %add.195), channel_id=1, source_target_pairs={{0,16},{2,18},{4,20},{6,22},{8,24},{10,26},{12,28},{14,30},{16,0},... | collective-permute-start | bytes 24584 | tf_op jit(solution)/shard_map/ppermute | solution.py:747
  140.3 4.5 %collective-permute-start.26 = (f32[16,128]{1,0:T(8,128)S(1)}, f32[16,128]{1,0:T(8,128)S(1)}, u32[]{:S(2)}, u32[]{:S(2)}) collective-permute-start(f32[16,128]{1,0:T(8,128)S(1)} %add.195), channel_id=1, source_target_pairs={{0,8},{2,10},{4,12},{6,14},{8,0},{10,2},{12,4},{14,6},{16,24},{18,... | collective-permute-start | bytes 24584 | tf_op jit(solution)/shard_map/ppermute | solution.py:747
  145.9 21.9 %collective-permute-start.29 = (f32[2,512,128]{2,1,0:T(8,128)S(1)}, f32[2,512,128]{2,1,0:T(8,128)S(1)}, u32[]{:S(2)}, u32[]{:S(2)}) collective-permute-start(f32[2,512,128]{2,1,0:T(8,128)S(1)} %get-tuple-element.61), channel_id=1, source_target_pairs={{8,1},{9,0},{10,3},{11,2},{0,5},{1,4},{2,7},{3,6},{4,9},{5,8},{6,1... | collective-permute-start | bytes 1572872 | tf_op jit(solution)/shard_map/ppermute | solution.py:756
  147.4 23.0 %collective-permute-start.30 = (f32[2,512,128]{2,1,0:T(8,128)S(1)}, f32[2,512,128]{2,1,0:T(8,128)S(1)}, u32[]{:S(2)}, u32[]{:S(2)}) collective-permute-start(f32[2,512,128]{2,1,0:T(8,128)S(1)} %get-tuple-element.62), channel_id=1, source_target_pairs={{8,0},{9,1},{10,2},{11,3},{0,4},{1,5},{2,6},{3,7},{4,8},{5,9},{6,1... | collective-permute-start | bytes 1572872 | tf_op jit(solution)/shard_map/ppermute | solution.py:756
